TPU v7x, 32 devices: a whole 2x2x4 slice. The times are simulated.
32 devices in a mesh: grp: 4 (over z), ctx: 2 (over y), wid: 4 (over x, core).
Axes of the slice: x: 2, y: 2, z: 4, core: 2. Of those that a mesh axis runs over, the one named last changes fastest.
Arguments:
- query: bfloat16 [256, 64, 128], P(None, 'wid'), may hold values from -64 to 64
- keys: bfloat16 [4, 512, 8, 128], P(None, ('grp', 'ctx'), 'wid'), may hold values from -64 to 64
- values: bfloat16 [4, 512, 8, 128], P(None, ('grp', 'ctx'), 'wid'), may hold values from -6 to 6
- lengths: int32 [4, 8], replicated, may hold values from 32 to 64
- query_pos: int32 [256], replicated, may hold values from 128 to 511
- resid: bfloat16 [256, 5120], P('wid', ('grp', 'ctx')), may hold values from -1.1953125 to 1.1953125
- out_weight: bfloat16 [8192, 5120], P('wid', ('grp', 'ctx')), may hold values from -0.0625 to 0.0625
- enc_weight: bfloat16 [5120, 24576], P('wid', ('grp', 'ctx')), may hold values from -0.078125 to 0.078125
- enc_bias: float32 [24576], P(('grp', 'ctx')), may hold values from -3 to 3
- dec_weight: bfloat16 [24576, 5120], P(('grp', 'ctx'), 'wid'), may hold values from -0.078125 to 0.078125
- dec_bias: float32 [5120], P('wid'), may hold values from -3 to 3
Outputs:
- layer_out: bfloat16 [256, 5120], P('wid', ('grp', 'ctx'))
- enc_grad: bfloat16 [5120, 24576], P('wid', ('grp', 'ctx'))
- enc_bias_grad: float32 [24576], P(('grp', 'ctx'))
- dec_grad: bfloat16 [24576, 5120], P(('grp', 'ctx'), 'wid')
- dec_bias_grad: float32 [5120], P('wid')
Inputs may be any that keep to these rules, and one draw needn't show every extreme that they name: `lengths`: live slots of a shard are its first ones.
All inputs are finite; a program needn't handle non-finite values.
Results may differ from a plain program's by a relative error of at most 0.024.
Values may be sent and summed in bfloat16 or wider, within the bound.
A program may use at most 128 MiB of HBM per device.

v0:
```python
import functools

import jax
import jax.numpy as jnp
from jax import lax
from jax.experimental import pallas as pl
from jax.experimental.pallas import tpu as pltpu
from jax.sharding import PartitionSpec as P

HD = 128
MESH = pl.DeviceIdType.MESH


def exchange_kernel(n, where, peer_id, gather, x_ref, out_ref, send_sem, recv_sem):
    me = where()
    peers = [lax.rem(me + step, n) for step in range(1, n)]
    barrier = pltpu.get_barrier_semaphore()
    for peer in peers:
        pl.semaphore_signal(barrier, inc=1, device_id=peer_id(peer), device_id_type=MESH)
    pl.semaphore_wait(barrier, n - 1)

    def copy_to(step, peer):
        return pltpu.make_async_remote_copy(
            src_ref=x_ref if gather else x_ref.at[peer],
            dst_ref=out_ref.at[me],
            send_sem=send_sem.at[step],
            recv_sem=recv_sem.at[me],
            device_id=peer_id(peer),
            device_id_type=MESH,
        )

    def copy_from(step, peer):
        return pltpu.make_async_remote_copy(
            src_ref=x_ref if gather else x_ref.at[peer],
            dst_ref=out_ref.at[peer],
            send_sem=send_sem.at[step],
            recv_sem=recv_sem.at[peer],
            device_id=peer_id(peer),
            device_id_type=MESH,
        )

    sends = [copy_to(step, peer) for step, peer in enumerate(peers)]
    for copy in sends:
        copy.start()
    out_ref[me] = x_ref[...] if gather else x_ref[me]
    for step, peer in enumerate(peers):
        copy_from(step, peer).wait_recv()
    for copy in sends:
        copy.wait_send()


def exchange(x, n, where, peer_id, gather, number):
    block = x.shape if gather else x.shape[1:]
    return pl.pallas_call(
        functools.partial(exchange_kernel, n, where, peer_id, gather),
        out_shape=jax.ShapeDtypeStruct((n,) + block, x.dtype),
        in_specs=[pl.BlockSpec(memory_space=pltpu.VMEM)],
        out_specs=pl.BlockSpec(memory_space=pltpu.VMEM),
        scratch_shapes=[pltpu.SemaphoreType.DMA((n,)), pltpu.SemaphoreType.DMA((n,))],
        compiler_params=pltpu.CompilerParams(
            collective_id=number, has_side_effects=True, vmem_limit_bytes=24 * 1024 * 1024
        ),
        name="exchange%d" % number,
    )(x)


class Groups:
    def __init__(self, sizes):
        ctx_n = sizes["ctx"]
        self.shards = (
            sizes["grp"] * ctx_n,
            lambda: lax.axis_index("grp") * ctx_n + lax.axis_index("ctx"),
            lambda p: {"grp": p // ctx_n, "ctx": lax.rem(p, ctx_n)},
        )
        self.wid = (sizes["wid"], lambda: lax.axis_index("wid"), lambda p: {"wid": p})
        self.low = (
            2,
            lambda: lax.rem(lax.axis_index("wid"), 2),
            lambda p: {"wid": (lax.axis_index("wid") // 2) * 2 + p},
        )
        self.high = (
            sizes["wid"] // 2,
            lambda: lax.axis_index("wid") // 2,
            lambda p: {"wid": p * 2 + lax.rem(lax.axis_index("wid"), 2)},
        )


def scatter_sum(x, group, number):
    n = group[0]
    parts = exchange(x.reshape((n, x.shape[0] // n) + x.shape[1:]), *group, False, number)
    return jnp.sum(parts.astype(jnp.float32), axis=0)


def gather_rows(x, group, number):
    whole = exchange(x, *group, True, number)
    return whole.reshape((whole.shape[0] * whole.shape[1],) + whole.shape[2:])


def attend(groups, query, keys, values, lengths, query_pos):
    seq_count, slot_count, kv_local, head_dim = keys.shape
    row_count, heads_local = query.shape[:2]
    group_size = heads_local // kv_local
    shards = groups.shards[0]
    pairs = seq_count * kv_local
    chunks = shards // pairs
    rows = row_count // seq_count // chunks
    pair = lax.axis_index(("grp", "ctx")) // chunks
    seq, head = pair // kv_local, lax.rem(pair, kv_local)
    row0 = seq * (row_count // seq_count) + lax.rem(lax.axis_index(("grp", "ctx")), chunks) * rows
    cache = jnp.concatenate([keys, values], axis=-1).transpose(0, 2, 1, 3)
    cache = cache.reshape(pairs, slot_count, 2 * head_dim)
    if chunks > 1:
        cache = jnp.repeat(cache, chunks, axis=0)
    cache = exchange(cache, *groups.shards, False, 0).reshape(shards * slot_count, 2 * head_dim)
    q = lax.dynamic_slice(query, (row0, head * group_size, 0), (rows, group_size, head_dim))
    live = lax.dynamic_index_in_dim(lengths, seq, 0, keepdims=False)
    before = jnp.arange(shards)[None, :] < jnp.arange(shards)[:, None]
    offset = jnp.sum(jnp.where(before, live[None, :], 0), axis=1)
    slot_ids = jnp.arange(slot_count, dtype=jnp.int32)
    key_pos = jnp.where(
        slot_ids[None, :] < live[:, None], offset[:, None] + slot_ids[None, :], jnp.int32(2**30)
    ).reshape(-1)
    position = lax.dynamic_slice_in_dim(query_pos, row0, rows, 0)
    visible = (key_pos[None, :] <= position[:, None])[:, None, :]
    scores = jnp.einsum(
        "rgd,td->rgt", q, cache[:, :head_dim], preferred_element_type=jnp.float32
    ) * HD ** (-0.5)
    peak = jnp.max(jnp.where(visible, scores, -1e30), axis=-1, keepdims=True)
    weights = jnp.where(visible, jnp.exp(scores - peak), 0.0)
    weight_sum = jnp.sum(weights, axis=-1, keepdims=True)
    weighted = jnp.einsum(
        "rgt,td->rgd", weights.astype(jnp.bfloat16), cache[:, head_dim:],
        preferred_element_type=jnp.float32,
    )
    mine = (weighted / weight_sum).astype(jnp.bfloat16).reshape(rows, group_size * head_dim)
    attention = exchange(mine, *groups.shards, True, 1)
    attention = attention.reshape(seq_count, kv_local, chunks, rows, group_size * head_dim)
    return attention.transpose(0, 2, 3, 1, 4).reshape(row_count, heads_local * head_dim)


def body(
    sizes,
    query,
    keys,
    values,
    lengths,
    query_pos,
    resid,
    out_weight,
    enc_weight,
    enc_bias,
    dec_weight,
    dec_bias,
):
    groups = Groups(sizes)
    row_count = query.shape[0]
    shard_pos = lax.axis_index(("grp", "ctx"))
    attention = attend(groups, query, keys, values, lengths, query_pos)
    projected = jnp.dot(attention, out_weight, preferred_element_type=jnp.float32)
    mixed = scatter_sum(projected.astype(jnp.bfloat16), groups.wid, 2)
    layer_out = (mixed + resid.astype(jnp.float32)).astype(jnp.bfloat16)
    rows, cols = layer_out.shape
    wid_n = sizes["wid"]
    wide = exchange(layer_out, *groups.shards, True, 3)
    wide = wide.reshape(wid_n, -1, rows, cols).transpose(0, 2, 1, 3).reshape(wid_n, rows, -1)
    block = exchange(wide, *groups.wid, False, 4).reshape(row_count, -1)
    enc_part = jnp.dot(block, enc_weight, preferred_element_type=jnp.float32)
    preact = scatter_sum(enc_part.astype(jnp.bfloat16), groups.low, 5).astype(jnp.bfloat16)
    preact = scatter_sum(preact, groups.high, 6) + enc_bias
    my_latents = (jax.nn.softplus(4.0 * preact) * 0.25).astype(jnp.bfloat16)
    latents = gather_rows(gather_rows(my_latents, groups.high, 7), groups.low, 8)
    row_scale = row_count ** (-0.5)
    recon = jnp.dot(latents, dec_weight, preferred_element_type=jnp.float32)
    recon = scatter_sum(recon.astype(jnp.bfloat16), groups.shards, 9)
    piece_len = recon.shape[0]
    target = lax.dynamic_slice_in_dim(block, shard_pos * piece_len, piece_len, 0).astype(
        jnp.float32
    )
    scaled_error = ((recon + dec_bias - target) * row_scale).astype(jnp.bfloat16)
    error_all = gather_rows(scaled_error, groups.shards, 10)
    dec_bias_grad = jnp.sum(error_all, axis=0, dtype=jnp.float32)
    latent_part = lax.dot_general(
        error_all, dec_weight, (((1,), (1,)), ((), ())), preferred_element_type=jnp.float32
    )
    dec_grad = lax.dot_general(
        latents, error_all, (((0,), (0,)), ((), ())), preferred_element_type=jnp.float32
    )
    latent_grad = scatter_sum(latent_part.astype(jnp.bfloat16), groups.low, 11).astype(jnp.bfloat16)
    latent_grad = scatter_sum(latent_grad, groups.high, 12)
    my_grad = (latent_grad * jax.nn.sigmoid(4.0 * preact)).astype(jnp.bfloat16)
    preact_grad = gather_rows(gather_rows(my_grad, groups.high, 13), groups.low, 14)
    enc_grad = lax.dot_general(
        block, preact_grad, (((0,), (0,)), ((), ())), preferred_element_type=jnp.float32
    ).astype(jnp.bfloat16)
    enc_bias_grad = jnp.sum(preact_grad, axis=0, dtype=jnp.float32)
    return (layer_out, enc_grad, enc_bias_grad, dec_grad.astype(jnp.bfloat16), dec_bias_grad)


def solution(mesh):
    placed = (
        P(None, "wid", None),
        P(None, ("grp", "ctx"), "wid", None),
        P(None, ("grp", "ctx"), "wid", None),
        P(),
        P(),
        P("wid", ("grp", "ctx")),
        P("wid", ("grp", "ctx")),
        P("wid", ("grp", "ctx")),
        P(("grp", "ctx")),
        P(("grp", "ctx"), "wid"),
        P("wid"),
    )
    return jax.shard_map(
        functools.partial(body, dict(mesh.shape)),
        mesh=mesh,
        in_specs=placed,
        out_specs=(
            P("wid", ("grp", "ctx")),
            P("wid", ("grp", "ctx")),
            P(("grp", "ctx")),
            P(("grp", "ctx"), "wid"),
            P("wid"),
        ),
        check_vma=False,
    )
```

profile of v0, /device:TPU:0, one launch (start us, length us, event | category | flops | bytes accessed | tf_op | source)
XLA Modules:
  0.0 214.4 jit_solution(17874746346797019179)
XLA Ops:
  0.6 0.0 copy-start
  0.7 1.4 maximum_bitcast_fusion
  2.1 10.9 %exchange0.1 = bf16[8,64,256]{2,1,0:T(8,128)(2,1)S(1)} custom-call(bf16[8,64,256]{2,1,0:T(8,128)(2,1)S(1)} %bitcast.67), custom_call_target="tpu_custom_call" | custom-call | tf_op jit(solution)/shard_map/exchange0/pallas_call | solution.py:54
  13.0 2.2 %convolution_multiply_fusion = f32[64,8,512]{2,1,0:T(8,128)} fusion(bf16[512,256]{1,0:T(8,128)(2,1)S(1)} %bitcast.69, bf16[256,16,128]{2,1,0:T(8,128)(2,1)} %param.11, s32[]{:T(128)S(6)} %select_n.51, s32[]{:T(128)S(6)} %select_n.52), kind=kOutput, calls=%fused_computation.15 | convolution fusion | flops 67371008 | bytes 1310728 | tf_op jit(solution)/shard_map/rgd,td->rgt/dot_general | solution.py:125
  15.2 0.7 fusion.17
  15.9 0.1 select_reduce_fusion.1
  16.0 0.1 add_select_fusion
  16.1 0.1 select_n.50
  16.1 0.1 dynamic_slice.14
  16.2 0.1 broadcast_compare_fusion
  16.3 2.1 fusion.19
  18.4 0.3 fusion.9
  18.7 20.8 %exchange1.1 = bf16[8,64,1024]{2,1,0:T(8,128)(2,1)S(1)} custom-call(bf16[64,1024]{1,0:T(8,128)(2,1)S(1)} %bitcast.71), custom_call_target="tpu_custom_call" | custom-call | tf_op jit(solution)/shard_map/exchange1/pallas_call | solution.py:54
  39.6 1.1 copy.22
  40.7 0.3 copy.25
  40.9 0.0 copy-done
  41.0 0.0 copy-start.13
  41.0 1.0 convolution_convert_fusion.5
  42.0 5.6 %exchange2.1 = bf16[4,64,640]{2,1,0:T(8,128)(2,1)S(1)} custom-call(bf16[4,64,640]{2,1,0:T(8,128)(2,1)S(1)} %bitcast.72), custom_call_target="tpu_custom_call" | custom-call | tf_op jit(solution)/shard_map/exchange2/pallas_call | solution.py:54
  47.6 0.0 copy-done.13
  47.7 0.0 copy-start.10
  47.7 21.4 %exchange3.1 = bf16[8,64,640]{2,1,0:T(8,128)(2,1)S(1)} custom-call(bf16[64,640]{1,0:T(8,128)(2,1)S(1)} %add_convert_fusion.x_ref), custom_call_target="tpu_custom_call" | custom-call | tf_op jit(solution)/shard_map/exchange3/pallas_call | solution.py:54
  69.1 0.7 copy.28
  69.8 1.3 reshape.135.x_ref
  71.1 1.1 copy-done.9
  72.1 9.0 %exchange4.1 = bf16[4,64,1280]{2,1,0:T(8,128)(2,1)S(1)} custom-call(bf16[4,64,1280]{2,1,0:T(8,128)(2,1)S(1)} %copy-done.9), custom_call_target="tpu_custom_call" | custom-call | tf_op jit(solution)/shard_map/exchange4/pallas_call | solution.py:54
  81.2 5.7 %convolution_convert_fusion.3 = bf16[256,3072]{1,0:T(8,128)(2,1)S(1)} fusion(bf16[256,1280]{1,0:T(8,128)(2,1)S(1)} %bitcast.57, bf16[1280,3072]{1,0:T(8,128)(2,1)} %param.18), kind=kOutput, calls=%fused_computation.4 | convolution fusion | flops 2014052352 | bytes 10092544 | tf_op jit(solution)/shard_map/dot_general | solution.py:167
  86.9 2.9 %exchange5.1 = bf16[2,128,3072]{2,1,0:T(8,128)(2,1)S(1)} custom-call(bf16[2,128,3072]{2,1,0:T(8,128)(2,1)S(1)} %bitcast.65), custom_call_target="tpu_custom_call" | custom-call | tf_op jit(solution)/shard_map/exchange5/pallas_call | solution.py:54
  89.8 0.0 copy-start.4
  89.8 1.1 copy-done.4
  91.0 2.8 %reduce_sum.99 = bf16[128,3072]{1,0:T(8,128)(2,1)} reduce(bf16[2,128,3072]{2,1,0:T(8,128)(2,1)} %copy-done.4, bf16[]{:T(256)} %constant.67.clone.1), dimensions={0}, to_apply=%region_4.5 | reduce | flops 393216 | bytes 2359298 | tf_op jit(solution)/shard_map/reduce_sum | solution.py:91
  93.8 1.1 copy-done.8
  94.9 11.4 %exchange6.1 = bf16[2,64,3072]{2,1,0:T(8,128)(2,1)S(1)} custom-call(bf16[2,64,3072]{2,1,0:T(8,128)(2,1)S(1)} %bitcast.61), custom_call_target="tpu_custom_call" | custom-call | tf_op jit(solution)/shard_map/exchange6/pallas_call | solution.py:54
  106.3 0.1 convert_reduce_fusion.2
  106.5 0.9 copy-done.11
  107.4 0.5 fusion.11.x_ref
  107.9 10.6 %exchange7.1 = bf16[2,64,3072]{2,1,0:T(8,128)(2,1)S(1)} custom-call(bf16[64,3072]{1,0:T(8,128)(2,1)S(1)} %fusion.11.x_ref), custom_call_target="tpu_custom_call" | custom-call | tf_op jit(solution)/shard_map/exchange7/pallas_call | solution.py:54
  118.5 2.3 %exchange8.1 = bf16[2,128,3072]{2,1,0:T(8,128)(2,1)S(1)} custom-call(bf16[128,3072]{1,0:T(8,128)(2,1)S(1)} %bitcast.62), custom_call_target="tpu_custom_call" | custom-call | tf_op jit(solution)/shard_map/exchange8/pallas_call | solution.py:54
  120.8 0.0 copy-start.1
  120.8 0.0 copy-start.15
  120.8 6.0 %convolution_convert_fusion.4 = bf16[256,1280]{1,0:T(8,128)(2,1)S(1)} fusion(bf16[256,3072]{1,0:T(8,128)(2,1)S(1)} %bitcast.52, bf16[3072,1280]{1,0:T(8,128)(2,1)} %param.20), kind=kOutput, calls=%fused_computation.6 | convolution fusion | flops 2013593600 | bytes 10092544 | tf_op jit(solution)/shard_map/dot_general | solution.py:173
  126.8 18.8 %exchange9.1 = bf16[8,32,1280]{2,1,0:T(8,128)(2,1)S(1)} custom-call(bf16[8,32,1280]{2,1,0:T(8,128)(2,1)S(1)} %bitcast.68), custom_call_target="tpu_custom_call" | custom-call | tf_op jit(solution)/shard_map/exchange9/pallas_call | solution.py:54
  145.6 0.1 convert_reduce_fusion.4
  145.7 0.0 copy-done.5
  145.7 0.0 copy-done.15
  145.8 18.1 %exchange10.1 = bf16[8,32,1280]{2,1,0:T(8,128)(2,1)S(1)} custom-call(bf16[32,1280]{1,0:T(8,128)(2,1)S(1)} %multiply_convert_fusion.1.x_ref), custom_call_target="tpu_custom_call" | custom-call | tf_op jit(solution)/shard_map/exchange10/pallas_call | solution.py:54
  163.9 5.6 %convolution_convert_fusion.2 = bf16[256,3072]{1,0:T(8,128)(2,1)S(1)} fusion(bf16[256,1280]{1,0:T(8,128)(2,1)S(1)} %bitcast.54, bf16[3072,1280]{1,0:T(8,128)(2,1)} %param.20), kind=kOutput, calls=%fused_computation.3 | convolution fusion | flops 2014052352 | bytes 10092544 | tf_op jit(solution)/shard_map/dot_general | solution.py:182
  169.6 2.3 %exchange11.1 = bf16[2,128,3072]{2,1,0:T(8,128)(2,1)S(1)} custom-call(bf16[2,128,3072]{2,1,0:T(8,128)(2,1)S(1)} %bitcast.66), custom_call_target="tpu_custom_call" | custom-call | tf_op jit(solution)/shard_map/exchange11/pallas_call | solution.py:54
  171.9 0.0 copy-start.3
  171.9 1.1 copy-done.3
  173.1 2.8 %reduce_sum.102 = bf16[128,3072]{1,0:T(8,128)(2,1)} reduce(bf16[2,128,3072]{2,1,0:T(8,128)(2,1)} %copy-done.3, bf16[]{:T(256)} %constant.67.clone.1), dimensions={0}, to_apply=%region_7.8 | reduce | flops 393216 | bytes 2359298 | tf_op jit(solution)/shard_map/reduce_sum | solution.py:91
  175.9 1.1 copy-done.7
  177.0 11.2 %exchange12.1 = bf16[2,64,3072]{2,1,0:T(8,128)(2,1)S(1)} custom-call(bf16[2,64,3072]{2,1,0:T(8,128)(2,1)S(1)} %bitcast.60), custom_call_target="tpu_custom_call" | custom-call | tf_op jit(solution)/shard_map/exchange12/pallas_call | solution.py:54
  188.2 0.1 convert_reduce_fusion.1
  188.4 0.0 copy-done.12
  188.4 0.0 copy-start.6
  188.4 0.2 multiply_convert_fusion.x_ref
  188.6 10.4 %exchange13.1 = bf16[2,64,3072]{2,1,0:T(8,128)(2,1)S(1)} custom-call(bf16[64,3072]{1,0:T(8,128)(2,1)S(1)} %multiply_convert_fusion.x_ref), custom_call_target="tpu_custom_call" | custom-call | tf_op jit(solution)/shard_map/exchange13/pallas_call | solution.py:54
  199.0 2.3 %exchange14.1 = bf16[2,128,3072]{2,1,0:T(8,128)(2,1)S(1)} custom-call(bf16[128,3072]{1,0:T(8,128)(2,1)S(1)} %bitcast.63), custom_call_target="tpu_custom_call" | custom-call | tf_op jit(solution)/shard_map/exchange14/pallas_call | solution.py:54
  201.3 5.5 %convolution_convert_fusion.1 = bf16[1280,3072]{1,0:T(8,128)(2,1)} fusion(bf16[256,1280]{1,0:T(8,128)(2,1)S(1)} %bitcast.59, bf16[256,3072]{1,0:T(8,128)(2,1)S(1)} %bitcast.51), kind=kOutput, calls=%fused_computation.2 | convolution fusion | flops 2017198080 | bytes 10092544 | tf_op jit(solution)/shard_map/dot_general | solution.py:192
  206.8 0.9 convert_reduce_fusion
  207.7 0.6 copy-done.2
  208.2 5.5 %convolution_convert_fusion = bf16[3072,1280]{1,0:T(8,128)(2,1)} fusion(bf16[256,3072]{1,0:T(8,128)(2,1)S(1)} %bitcast.53, bf16[256,1280]{1,0:T(8,128)(2,1)S(1)} %bitcast.55), kind=kOutput, calls=%fused_computation.1 | convolution fusion | flops 2017198080 | bytes 10092544 | tf_op jit(solution)/shard_map/dot_general | solution.py:185
  213.7 0.7 convert_reduce_fusion.3
  (19 shorter events, 0.2 us)
Async XLA Ops:
  0.6 40.3 %copy-start = (bf16[2048,640]{1,0:T(8,128)(2,1)S(1)}, bf16[2048,640]{1,0:T(8,128)(2,1)}, u32[]{:S(2)}) copy-start(bf16[2048,640]{1,0:T(8,128)(2,1)} %param.17) | copy-start | bytes 7864324
  0.6 15.5 %copy-start.16 = (s32[256]{0:T(256)S(1)}, s32[256]{0:T(256)}, u32[]{:S(2)}) copy-start(s32[256]{0:T(256)} %param.15) | copy-start | bytes 3076
  41.0 6.7 %copy-start.13 = (bf16[64,640]{1,0:T(8,128)(2,1)S(1)}, bf16[64,640]{1,0:T(8,128)(2,1)}, u32[]{:S(2)}) copy-start(bf16[64,640]{1,0:T(8,128)(2,1)} %param.16) | copy-start | bytes 245764
  47.7 39.3 %copy-start.10 = (bf16[64,640]{1,0:T(8,128)(2,1)}, bf16[64,640]{1,0:T(8,128)(2,1)S(1)}, u32[]{:S(2)}) copy-start(bf16[64,640]{1,0:T(8,128)(2,1)S(1)} %add_convert_fusion.x_ref) | copy-start | bytes 245764
  71.1 1.1 copy-start.9
  81.2 64.6 %copy-start.5 = (bf16[4,64,1280]{2,1,0:T(8,128)(2,1)}, bf16[4,64,1280]{2,1,0:T(8,128)(2,1)S(1)}, u32[]{:S(2)}) copy-start(bf16[4,64,1280]{2,1,0:T(8,128)(2,1)S(1)} %exchange4.1) | copy-start | bytes 1966084
  89.8 1.1 copy-start.4
  90.9 16.4 %copy-start.14 = (f32[3072]{0:T(1024)S(1)}, f32[3072]{0:T(1024)}, u32[]{:S(2)}) copy-start(f32[3072]{0:T(1024)} %param.19) | copy-start | bytes 36868
  93.8 1.1 copy-start.8
  106.5 0.9 copy-start.11
  120.8 6.0 %copy-start.1 = (bf16[2,128,3072]{2,1,0:T(8,128)(2,1)}, bf16[2,128,3072]{2,1,0:T(8,128)(2,1)S(1)}, u32[]{:S(2)}) copy-start(bf16[2,128,3072]{2,1,0:T(8,128)(2,1)S(1)} %exchange8.1) | copy-start | bytes 4718596
  120.8 24.9 %copy-start.15 = (f32[1280]{0:T(1024)S(1)}, f32[1280]{0:T(1024)}, u32[]{:S(2)}) copy-start(f32[1280]{0:T(1024)} %param.21) | copy-start | bytes 15364
  171.9 1.1 copy-start.3
  175.9 1.1 copy-start.7
  177.0 11.3 %copy-start.12 = (f32[64,3072]{1,0:T(8,128)S(1)}, f32[64,3072]{1,0:T(8,128)}, u32[]{:S(2)}) copy-start(f32[64,3072]{1,0:T(8,128)} %copy-done.11) | copy-start | bytes 2359300
  188.4 13.0 %copy-start.6 = (bf16[4,64,1280]{2,1,0:T(8,128)(2,1)S(1)}, bf16[4,64,1280]{2,1,0:T(8,128)(2,1)}, u32[]{:S(2)}) copy-start(bf16[4,64,1280]{2,1,0:T(8,128)(2,1)} %copy-done.5) | copy-start | bytes 1966084
  206.8 1.4 copy-start.2
where the time goes:
time: 217 us; the launch traced here: 214 us
  Pallas kernels  158 us (73%)
  matrix products  31.8 us (15%)
  other arithmetic  12.1 us (6%)
  local copies, waits for them, and re-layouts  11.3 us (5%)
    pallas_call x15, Pallas kernels, exchange(): pl.pallas_call(functools.partial(exchange_kernel, n, where, peer_id, gath...  158 us
    unnamed x36, local copies, waits for them, and re-layouts  7.41 us
    reduce_sum x6, other arithmetic, scatter_sum(): return jnp.sum(parts.astype(jnp.float32), axis=0)  6 us
    dot_general x1, matrix products, body(): recon = jnp.dot(latents, dec_weight, preferred_element_type=jnp.float32)  5.99 us
    dot_general x1, matrix products, body(): enc_part = jnp.dot(block, enc_weight, preferred_element_type=jnp.float32)  5.73 us
    dot_general x1, matrix products, body(): lax.dot_general(error_all, dec_weight, (((1,), (1,)), ((), ())), preferre...  5.65 us
    dot_general x1, matrix products, body(): lax.dot_general(latents, error_all, (((0,), (0,)), ((), ())), preferred_e...  5.5 us
    dot_general x1, matrix products, body(): lax.dot_general(block, preact_grad, (((0,), (0,)), ((), ())), preferred_e...  5.46 us

commit v1 on v0

--- a/solution.py
+++ b/solution.py
@@ -94,6 +94,361 @@
 def gather_rows(x, group, number):
     whole = exchange(x, *group, True, number)
     return whole.reshape((whole.shape[0] * whole.shape[1],) + whole.shape[2:])
+
+
+def local_copy(src, dst, sem):
+    return pltpu.make_async_copy(src, dst, sem)
+
+
+def rows_at(start, size):
+    return pl.ds(pl.multiple_of(start, 16), size)
+
+
+class Plan:
+    def __init__(self, sizes, row_count, width, latents):
+        self.grp, self.ctx, self.wid = sizes["grp"], sizes["ctx"], sizes["wid"]
+        self.high = self.wid // 2
+        self.row_count, self.width, self.latents = row_count, width, latents
+        self.streams = 2
+        self.rows = row_count // self.streams
+        self.half = self.rows // 2
+        self.quarter = self.rows // self.wid
+        self.side = self.rows // self.ctx
+        self.piece = self.side // self.grp
+
+    def fits(self):
+        return (
+            self.wid % 2 == 0
+            and self.row_count % self.streams == 0
+            and self.rows % (16 * self.wid) == 0
+            and self.rows % (16 * self.grp * self.ctx) == 0
+            and self.width % 256 == 0
+            and self.latents % 512 == 0
+        )
+
+
+def middle_kernel(
+    plan, block, enc_bias, dec_bias, enc_hbm, dec_hbm, lat, err, pgrad,
+    enc_w, dec_w, part, pair_in, pair_sum, high_in, factor, recon, side_in, side_sum, piece_in,
+    load_sem, pair_sem, high_sem, gather_sem, relay_sem, side_sem, piece_sem, spread_sem, cross_sem,
+):
+    p = plan
+    g, c, w = lax.axis_index("grp"), lax.axis_index("ctx"), lax.axis_index("wid")
+    low, high = lax.rem(w, 2), w // 2
+    partner = {"wid": w + 1 - 2 * low}
+    highs = [lax.rem(high + s, p.high) for s in range(1, p.high)]
+    ctxs = [lax.rem(c + s, p.ctx) for s in range(1, p.ctx)]
+    grps = [lax.rem(g + s, p.grp) for s in range(1, p.grp)]
+    highs_from = [lax.rem(high + p.high - s, p.high) for s in range(1, p.high)]
+    grps_from = [lax.rem(g + p.grp - s, p.grp) for s in range(1, p.grp)]
+    to_high = lambda h: {"wid": h * 2 + low}
+    to_ctx = lambda q: {"ctx": q}
+    to_grp = lambda q: {"grp": q}
+    peers = [partner] + [to_high(h) for h in highs] + [to_ctx(q) for q in ctxs] + [to_grp(q) for q in grps]
+
+    lat_step = 512
+    enc_steps = p.latents // lat_step
+    dec_rows = p.latents // 2
+    loads = [
+        local_copy(enc_hbm.at[:, pl.ds(j * lat_step, lat_step)], enc_w.at[:, pl.ds(j * lat_step, lat_step)], load_sem.at[j])
+        for j in range(enc_steps)
+    ]
+    late_loads = [
+        local_copy(dec_hbm.at[pl.ds(j * dec_rows, dec_rows)], dec_w.at[pl.ds(j * dec_rows, dec_rows)], load_sem.at[enc_steps + j])
+        for j in range(2)
+    ]
+    for copy in loads + late_loads:
+        copy.start()
+    barrier = pltpu.get_barrier_semaphore()
+    for peer in peers:
+        pl.semaphore_signal(barrier, inc=1, device_id=peer, device_id_type=MESH)
+    pl.semaphore_wait(barrier, len(peers))
+
+    pending = []
+
+    def send(src, dst, sem, index, peer):
+        copy = pltpu.make_async_remote_copy(
+            src_ref=src, dst_ref=dst, send_sem=sem.at[(0,) + index], recv_sem=sem.at[(1,) + index],
+            device_id=peer, device_id_type=MESH,
+        )
+        copy.start()
+        pending.append(copy)
+
+    def arrived(ref, sem, index, peer):
+        pltpu.make_async_remote_copy(
+            src_ref=ref, dst_ref=ref, send_sem=sem.at[(0,) + index], recv_sem=sem.at[(1,) + index],
+            device_id=peer, device_id_type=MESH,
+        ).wait_recv()
+
+    def quarter_row(t, lo, hi):
+        return t * p.rows + (lo * p.high + hi) * p.quarter
+
+    def piece_row(t, q, r):
+        return t * p.rows + q * p.side + r * p.piece
+
+    def pair_send(k, t):
+        there = part.at[k, rows_at(t * p.rows + (1 - low) * p.half, p.half)]
+        send(there, pair_in.at[k, t], pair_sem, (k, t), partner)
+
+    def pair_add(k, t):
+        arrived(pair_in.at[k, t], pair_sem, (k, t), partner)
+
+        def step(i, carry):
+            r = pl.multiple_of(i * 16, 16)
+            mine = part[k, rows_at(t * p.rows + low * p.half + r, 16)].astype(jnp.float32)
+            theirs = pair_in[k, t, pl.ds(r, 16)].astype(jnp.float32)
+            pair_sum[k, t, pl.ds(r, 16)] = (mine + theirs).astype(jnp.bfloat16)
+            return carry
+
+        lax.fori_loop(0, p.half // 16, step, 0)
+        for s, h in enumerate(highs):
+            send(pair_sum.at[k, t, rows_at(h * p.quarter, p.quarter)], high_in.at[k, t, s], high_sem, (k, t, s), to_high(h))
+
+    def high_sum(k, t, r):
+        total = pair_sum[k, t, rows_at(high * p.quarter + r, 16)].astype(jnp.float32)
+        for s in range(len(highs)):
+            total = total + high_in[k, t, s, pl.ds(r, 16)].astype(jnp.float32)
+        return total
+
+    def publish(k, t, out):
+        mine = out.at[rows_at(quarter_row(t, low, high), p.quarter)]
+        for s, h in enumerate(highs):
+            send(mine, mine, gather_sem, (k, t, s + 1), to_high(h))
+        send(mine, mine, gather_sem, (k, t, 0), partner)
+
+    def activate(t):
+        for s, h in enumerate(highs):
+            arrived(high_in.at[0, t, s], high_sem, (0, t, s), to_high(h))
+
+        def step(i, carry):
+            r = pl.multiple_of(i * 16, 16)
+            z = 4.0 * (high_sum(0, t, r) + enc_bias[...])
+            e = jnp.exp(-jnp.abs(z))
+            lat[rows_at(quarter_row(t, low, high) + r, 16)] = (
+                (jnp.maximum(z, 0.0) + jnp.log1p(e)) * 0.25
+            ).astype(jnp.bfloat16)
+            factor[t, pl.ds(r, 16)] = jnp.where(z >= 0.0, 1.0, e) / (1.0 + e)
+            return carry
+
+        lax.fori_loop(0, p.quarter // 16, step, 0)
+        publish(0, t, lat)
+
+    def cotangent(t):
+        for s, h in enumerate(highs):
+            arrived(high_in.at[1, t, s], high_sem, (1, t, s), to_high(h))
+
+        def step(i, carry):
+            r = pl.multiple_of(i * 16, 16)
+            pgrad[rows_at(quarter_row(t, low, high) + r, 16)] = (
+                high_sum(1, t, r) * factor[t, pl.ds(r, 16)]
+            ).astype(jnp.bfloat16)
+            return carry
+
+        lax.fori_loop(0, p.quarter // 16, step, 0)
+        publish(1, t, pgrad)
+
+    def relay(k, t, out):
+        for s, h in enumerate(highs_from):
+            theirs = out.at[rows_at(quarter_row(t, low, h), p.quarter)]
+            arrived(theirs, gather_sem, (k, t, s + 1), to_high(h))
+            send(theirs, theirs, relay_sem, (k, t, s), partner)
+
+    def collected(k, t, out):
+        arrived(out.at[rows_at(quarter_row(t, 1 - low, high), p.quarter)], gather_sem, (k, t, 0), partner)
+        for s, h in enumerate(highs):
+            arrived(out.at[rows_at(quarter_row(t, 1 - low, h), p.quarter)], relay_sem, (k, t, s), partner)
+
+    def encode(t):
+        rows = pl.ds(t * p.rows, p.rows)
+        for j in range(enc_steps):
+            if t == 0:
+                loads[j].wait()
+            cols = pl.ds(j * lat_step, lat_step)
+            part[0, rows, cols] = jnp.dot(
+                block[rows, :], enc_w[:, cols], preferred_element_type=jnp.float32
+            ).astype(jnp.bfloat16)
+        pair_send(0, t)
+
+    def decode(t):
+        collected(0, t, lat)
+        if t == 0:
+            for copy in late_loads:
+                copy.wait()
+        rows = pl.ds(t * p.rows, p.rows)
+
+        def step(j, carry):
+            cols = pl.ds(pl.multiple_of(j * 256, 256), 256)
+            recon[rows, cols] = jnp.dot(
+                lat[rows, :], dec_w[:, cols], preferred_element_type=jnp.float32
+            ).astype(jnp.bfloat16)
+            return carry
+
+        lax.fori_loop(0, p.width // 256, step, 0)
+        for s, q in enumerate(ctxs):
+            send(recon.at[rows_at(piece_row(t, q, 0), p.side)], side_in.at[t, s], side_sem, (t, s), to_ctx(q))
+
+    def side_add(t):
+        for s, q in enumerate(ctxs):
+            arrived(side_in.at[t, s], side_sem, (t, s), to_ctx(q))
+
+        def step(i, carry):
+            r = pl.multiple_of(i * 16, 16)
+            total = recon[rows_at(piece_row(t, c, 0) + r, 16)].astype(jnp.float32)
+            for s in range(len(ctxs)):
+                total = total + side_in[t, s, pl.ds(r, 16)].astype(jnp.float32)
+            side_sum[t, pl.ds(r, 16)] = total.astype(jnp.bfloat16)
+            return carry
+
+        lax.fori_loop(0, p.side // 16, step, 0)
+        for s, q in enumerate(grps):
+            send(side_sum.at[t, rows_at(q * p.piece, p.piece)], piece_in.at[t, s], piece_sem, (t, s), to_grp(q))
+
+    def error(t):
+        for s, q in enumerate(grps):
+            arrived(piece_in.at[t, s], piece_sem, (t, s), to_grp(q))
+
+        def step(i, carry):
+            r = pl.multiple_of(i * 16, 16)
+            total = side_sum[t, rows_at(g * p.piece + r, 16)].astype(jnp.float32)
+            for s in range(len(grps)):
+                total = total + piece_in[t, s, pl.ds(r, 16)].astype(jnp.float32)
+            rows = rows_at(piece_row(t, c, g) + r, 16)
+            wanted = block[rows].astype(jnp.float32)
+            err[rows] = ((total + dec_bias[...] - wanted) * p.row_count ** (-0.5)).astype(jnp.bfloat16)
+            return carry
+
+        lax.fori_loop(0, p.piece // 16, step, 0)
+        mine = err.at[rows_at(piece_row(t, c, g), p.piece)]
+        for s, q in enumerate(grps):
+            send(mine, mine, spread_sem, (t, s), to_grp(q))
+        for s, q in enumerate(ctxs):
+            send(mine, mine, cross_sem, (t, s, 0), to_ctx(q))
+
+    def error_relay(t):
+        for i, r in enumerate(grps_from):
+            theirs = err.at[rows_at(piece_row(t, c, r), p.piece)]
+            arrived(theirs, spread_sem, (t, i), to_grp(r))
+            for s, q in enumerate(ctxs):
+                send(theirs, theirs, cross_sem, (t, s, i + 1), to_ctx(q))
+
+    def back(t):
+        for s, q in enumerate(ctxs):
+            for i, r in enumerate([g] + grps):
+                arrived(err.at[rows_at(piece_row(t, q, r), p.piece)], cross_sem, (t, s, i), to_ctx(q))
+        rows = pl.ds(t * p.rows, p.rows)
+
+        def step(j, carry):
+            cols = pl.ds(pl.multiple_of(j * lat_step, lat_step), lat_step)
+            part[1, rows, cols] = lax.dot_general(
+                err[rows, :], dec_w[cols, :], (((1,), (1,)), ((), ())), preferred_element_type=jnp.float32
+            ).astype(jnp.bfloat16)
+            return carry
+
+        lax.fori_loop(0, enc_steps, step, 0)
+        pair_send(1, t)
+
+    stages = [
+        lambda: encode(0),
+        lambda: encode(1),
+        lambda: pair_add(0, 0),
+        lambda: pair_add(0, 1),
+        lambda: activate(0),
+        lambda: activate(1),
+        lambda: relay(0, 0, lat),
+        lambda: decode(0),
+        lambda: relay(0, 1, lat),
+        lambda: decode(1),
+        lambda: side_add(0),
+        lambda: side_add(1),
+        lambda: error(0),
+        lambda: error(1),
+        lambda: error_relay(0),
+        lambda: back(0),
+        lambda: error_relay(1),
+        lambda: pair_add(1, 0),
+        lambda: back(1),
+        lambda: pair_add(1, 1),
+        lambda: cotangent(0),
+        lambda: cotangent(1),
+        lambda: relay(1, 0, pgrad),
+        lambda: relay(1, 1, pgrad),
+        lambda: collected(1, 0, pgrad),
+        lambda: collected(1, 1, pgrad),
+    ]
+    for stage in stages:
+        stage()
+    for copy in pending:
+        copy.wait_send()
+
+
+def middle(plan, block, enc_weight, enc_bias, dec_weight, dec_bias, number):
+    p = plan
+    low = jnp.bfloat16
+    vmem = pl.BlockSpec(memory_space=pltpu.VMEM)
+    hbm = pl.BlockSpec(memory_space=pl.ANY)
+    n, highs, ctxs, grps = p.streams, p.high - 1, p.ctx - 1, p.grp - 1
+    dma = pltpu.SemaphoreType.DMA
+    return pl.pallas_call(
+        functools.partial(middle_kernel, p),
+        out_shape=(
+            jax.ShapeDtypeStruct((p.row_count, p.latents), low),
+            jax.ShapeDtypeStruct((p.row_count, p.width), low),
+            jax.ShapeDtypeStruct((p.row_count, p.latents), low),
+        ),
+        in_specs=[vmem, vmem, vmem, hbm, hbm],
+        out_specs=(vmem, vmem, vmem),
+        scratch_shapes=[
+            pltpu.VMEM((p.width, p.latents), low),
+            pltpu.VMEM((p.latents, p.width), low),
+            pltpu.VMEM((2, p.row_count, p.latents), low),
+            pltpu.VMEM((2, n, p.half, p.latents), low),
+            pltpu.VMEM((2, n, p.half, p.latents), low),
+            pltpu.VMEM((2, n, highs, p.quarter, p.latents), low),
+            pltpu.VMEM((n, p.quarter, p.latents), jnp.float32),
+            pltpu.VMEM((p.row_count, p.width), low),
+            pltpu.VMEM((n, ctxs, p.side, p.width), low),
+            pltpu.VMEM((n, p.side, p.width), low),
+            pltpu.VMEM((n, grps, p.piece, p.width), low),
+            dma((p.latents // 512 + 2,)),
+            dma((2, 2, n)),
+            dma((2, 2, n, highs)),
+            dma((2, 2, n, highs + 1)),
+            dma((2, 2, n, highs)),
+            dma((2, n, ctxs)),
+            dma((2, n, grps)),
+            dma((2, n, grps)),
+            dma((2, n, ctxs, grps + 1)),
+        ],
+        compiler_params=pltpu.CompilerParams(
+            collective_id=number, has_side_effects=True, vmem_limit_bytes=60 * 1024 * 1024
+        ),
+        name="middle",
+    )(block, enc_bias.reshape(1, -1), dec_bias.reshape(1, -1), enc_weight, dec_weight)
+
+
+def outer_kernel(x_ref, y_ref, out_ref, sum_ref):
+    @pl.when(pl.program_id(0) == 0)
+    def _():
+        sum_ref[...] = jnp.sum(y_ref[...].astype(jnp.float32), axis=0, keepdims=True)
+
+    out_ref[...] = lax.dot_general(
+        x_ref[...], y_ref[...], (((0,), (0,)), ((), ())), preferred_element_type=jnp.float32
+    ).astype(out_ref.dtype)
+
+
+def outer(x, y, step, name):
+    rows, m = x.shape
+    n = y.shape[1]
+    out, total = pl.pallas_call(
+        outer_kernel,
+        grid=(m // step,),
+        in_specs=[pl.BlockSpec((rows, step), lambda i: (0, i)), pl.BlockSpec((rows, n), lambda i: (0, 0))],
+        out_specs=(pl.BlockSpec((step, n), lambda i: (i, 0)), pl.BlockSpec((1, n), lambda i: (0, 0))),
+        out_shape=(jax.ShapeDtypeStruct((m, n), jnp.bfloat16), jax.ShapeDtypeStruct((1, n), jnp.float32)),
+        compiler_params=pltpu.CompilerParams(vmem_limit_bytes=32 * 1024 * 1024),
+        name=name,
+    )(x, y)
+    return out, total.reshape(n)
 
 
 def attend(groups, query, keys, values, lengths, query_pos):
@@ -164,6 +519,14 @@
     wide = exchange(layer_out, *groups.shards, True, 3)
     wide = wide.reshape(wid_n, -1, rows, cols).transpose(0, 2, 1, 3).reshape(wid_n, rows, -1)
     block = exchange(wide, *groups.wid, False, 4).reshape(row_count, -1)
+    plan = Plan(sizes, row_count, block.shape[1], enc_weight.shape[1])
+    if plan.fits():
+        latents, error_all, preact_grad = middle(
+            plan, block, enc_weight, enc_bias, dec_weight, dec_bias, 5
+        )
+        dec_grad, dec_bias_grad = outer(latents, error_all, 256, "dec_outer")
+        enc_grad, enc_bias_grad = outer(block, preact_grad, 128, "enc_outer")
+        return (layer_out, enc_grad, enc_bias_grad, dec_grad, dec_bias_grad)
     enc_part = jnp.dot(block, enc_weight, preferred_element_type=jnp.float32)
     preact = scatter_sum(enc_part.astype(jnp.bfloat16), groups.low, 5).astype(jnp.bfloat16)
     preact = scatter_sum(preact, groups.high, 6) + enc_bias

time: 217 us -> 182 us (0.84); the launches traced: 214 us -> 182 us
  matrix products: 31.8 us -> 2.52 us
  other arithmetic: 12.1 us -> 2.71 us
  Pallas kernels: 158 us -> 165 us
    pallas_call x0 -> x3, Pallas kernels: none -> 97.3 us  [the longest x1 82.1 us: middle(): pl.pallas_call(functools.partial(middle_kernel, p), out_shape=(jax.ShapeD...]
    pallas_call x15 -> x5, Pallas kernels: 158 us -> 67.8 us  [exchange(): pl.pallas_call(functools.partial(exchange_kernel, n, where, peer_id, gath...]
    dot_general x5 -> x0, matrix products: 28.3 us -> none  [the longest x1 5.99 us: body(): recon = jnp.dot(latents, dec_weight, preferred_element_type=jnp.float32)]
    reduce_sum x6 -> x1, other arithmetic: 6 us -> 0.04 us  [scatter_sum(): return jnp.sum(parts.astype(jnp.float32), axis=0)]
    unnamed x36 -> x18, local copies, waits for them, and re-layouts: 7.41 us -> 2.67 us
where the time goes in v1:
time: 182 us
  Pallas kernels  165 us (91%)
  local copies, waits for them, and re-layouts  10.5 us (6%)
  other arithmetic  2.71 us (1%)
  matrix products  2.52 us (1%)
    pallas_call x1, Pallas kernels, middle(): pl.pallas_call(functools.partial(middle_kernel, p), out_shape=(jax.ShapeD...  82.1 us
    pallas_call x5, Pallas kernels, exchange(): pl.pallas_call(functools.partial(exchange_kernel, n, where, peer_id, gath...  67.8 us
    pallas_call x2, Pallas kernels, outer(): pl.pallas_call(outer_kernel, grid=(m // step,), in_specs=[pl.BlockSpec((r...  15.2 us
    reshape x2, local copies, waits for them, and re-layouts, body(): wide.reshape(wid_n, -1, rows, cols).transpose(0, 2, 1, 3)  3.73 us

profile of v1, /device:TPU:0, one launch (start us, length us, event | category | flops | bytes accessed | tf_op | source)
XLA Modules:
  0.0 181.6 jit_solution(8940193663021237286)
XLA Ops:
  0.6 0.0 copy-start
  0.7 0.8 dynamic-slice_bitcast_fusion
  1.5 0.1 select_reduce_fusion.1
  1.6 0.8 dynamic_slice.11
  2.4 0.1 add_select_fusion
  2.5 0.1 select_n.43
  2.5 1.3 reshape.118.dec_bias
  3.8 0.1 broadcast_compare_fusion
  3.9 1.2 maximum_bitcast_fusion
  5.2 10.9 %exchange0.1 = bf16[8,64,256]{2,1,0:T(8,128)(2,1)S(1)} custom-call(bf16[8,64,256]{2,1,0:T(8,128)(2,1)S(1)} %bitcast.37), custom_call_target="tpu_custom_call" | custom-call | tf_op jit(solution)/shard_map/exchange0/pallas_call | solution.py:54
  16.1 1.2 convolution_multiply_fusion
  17.3 0.5 fusion.16
  17.8 0.3 fusion.9
  18.1 20.8 %exchange1.1 = bf16[8,64,1024]{2,1,0:T(8,128)(2,1)S(1)} custom-call(bf16[64,1024]{1,0:T(8,128)(2,1)S(1)} %bitcast.40), custom_call_target="tpu_custom_call" | custom-call | tf_op jit(solution)/shard_map/exchange1/pallas_call | solution.py:54
  39.0 1.1 copy.22
  40.1 0.3 copy.25
  40.4 0.0 copy-done
  40.4 0.0 copy-start.7
  40.4 1.0 convolution_convert_fusion
  41.4 5.6 %exchange2.1 = bf16[4,64,640]{2,1,0:T(8,128)(2,1)S(1)} custom-call(bf16[4,64,640]{2,1,0:T(8,128)(2,1)S(1)} %bitcast.41), custom_call_target="tpu_custom_call" | custom-call | tf_op jit(solution)/shard_map/exchange2/pallas_call | solution.py:54
  47.0 0.0 copy-done.7
  47.1 0.0 copy-start.6
  47.1 21.4 %exchange3.1 = bf16[8,64,640]{2,1,0:T(8,128)(2,1)S(1)} custom-call(bf16[64,640]{1,0:T(8,128)(2,1)S(1)} %add_convert_fusion.x_ref), custom_call_target="tpu_custom_call" | custom-call | tf_op jit(solution)/shard_map/exchange3/pallas_call | solution.py:54
  68.5 1.5 copy.28
  70.0 2.2 %reshape.115.x_ref = bf16[4,64,1280]{2,1,0:T(8,128)(2,1)S(1)} reshape(bf16[4,64,2,640]{3,2,1,0:T(2,128)(2,1)} %bitcast.43) | data formatting | bytes 1310720 | tf_op jit(solution)/shard_map/reshape | solution.py:520
  72.3 9.0 %exchange4.1 = bf16[4,64,1280]{2,1,0:T(8,128)(2,1)S(1)} custom-call(bf16[4,64,1280]{2,1,0:T(8,128)(2,1)S(1)} %reshape.115.x_ref), custom_call_target="tpu_custom_call" | custom-call | tf_op jit(solution)/shard_map/exchange4/pallas_call | solution.py:54
  81.3 0.0 copy-start.1
  81.3 0.8 copy-done.1
  82.2 0.0 copy-start.2
  82.2 82.1 %middle.1 = (bf16[256,3072]{1,0:T(8,128)(2,1)}, bf16[256,1280]{1,0:T(8,128)(2,1)}, bf16[256,3072]{1,0:T(8,128)(2,1)}) custom-call(bf16[256,1280]{1,0:T(8,128)(2,1)} %bitcast.33, f32[1,3072]{1,0:T(1,128)} %bitcast.46, f32[1,1280]{1,0:T(1,128)} %reshape.118.dec_bias, bf16[1280,3072]{1,0:T(8,128)(2,1)} %enc_hbm.1, bf16[3072,1280]{1,0:T(8,128)(2,1)} %dec_hbm.1), custom_call_target="tpu_custom_call" | custom-call | tf_op jit(solution)/shard_map/middle/pallas_call | solution.py:391
  164.3 0.0 copy-done.6
  164.3 0.0 copy-start.3
  164.3 0.0 copy-done.2
  164.3 0.0 copy-start.4
  164.3 1.5 copy-done.4
  165.8 0.0 copy-start.5
  165.8 7.2 %enc_outer.1 = (bf16[1280,3072]{1,0:T(8,128)(2,1)}, f32[1,3072]{1,0:T(1,128)}) custom-call(bf16[256,1280]{1,0:T(8,128)(2,1)S(1)} %bitcast.34, bf16[256,3072]{1,0:T(8,128)(2,1)S(1)} %copy-done.4), custom_call_target="tpu_custom_call" | custom-call | tf_op jit(solution)/shard_map/enc_outer/pallas_call | solution.py:442
  173.0 0.0 copy-done.3
  173.0 0.0 copy-done.5
  173.0 8.0 %dec_outer.1 = (bf16[3072,1280]{1,0:T(8,128)(2,1)}, f32[1,1280]{1,0:T(1,128)S(1)}) custom-call(bf16[256,3072]{1,0:T(8,128)(2,1)S(1)} %copy-done.3, bf16[256,1280]{1,0:T(8,128)(2,1)S(1)} %copy-done.5), custom_call_target="tpu_custom_call" | custom-call | tf_op jit(solution)/shard_map/dec_outer/pallas_call | solution.py:442
  181.0 0.6 reduce
  (4 shorter events, 0.1 us)
Async XLA Ops:
  0.6 39.7 %copy-start = (bf16[2048,640]{1,0:T(8,128)(2,1)S(1)}, bf16[2048,640]{1,0:T(8,128)(2,1)}, u32[]{:S(2)}) copy-start(bf16[2048,640]{1,0:T(8,128)(2,1)} %param.17) | copy-start | bytes 7864324
  40.4 6.7 %copy-start.7 = (bf16[64,640]{1,0:T(8,128)(2,1)S(1)}, bf16[64,640]{1,0:T(8,128)(2,1)}, u32[]{:S(2)}) copy-start(bf16[64,640]{1,0:T(8,128)(2,1)} %param.16) | copy-start | bytes 245764
  47.1 117.2 %copy-start.6 = (bf16[64,640]{1,0:T(8,128)(2,1)}, bf16[64,640]{1,0:T(8,128)(2,1)S(1)}, u32[]{:S(2)}) copy-start(bf16[64,640]{1,0:T(8,128)(2,1)S(1)} %add_convert_fusion.x_ref) | copy-start | bytes 245764
  81.3 0.8 copy-start.1
  82.2 82.1 %copy-start.2 = (bf16[4,64,1280]{2,1,0:T(8,128)(2,1)S(1)}, bf16[4,64,1280]{2,1,0:T(8,128)(2,1)}, u32[]{:S(2)}) copy-start(bf16[4,64,1280]{2,1,0:T(8,128)(2,1)} %copy-done.1) | copy-start | bytes 1966084
  164.3 8.7 %copy-start.3 = (bf16[256,3072]{1,0:T(8,128)(2,1)S(1)}, bf16[256,3072]{1,0:T(8,128)(2,1)}, u32[]{:S(2)}) copy-start(bf16[256,3072]{1,0:T(8,128)(2,1)} %get-tuple-element.15.x_ref) | copy-start | bytes 4718596
  164.3 1.5 copy-start.4
  165.8 7.2 %copy-start.5 = (bf16[256,1280]{1,0:T(8,128)(2,1)S(1)}, bf16[256,1280]{1,0:T(8,128)(2,1)}, u32[]{:S(2)}) copy-start(bf16[256,1280]{1,0:T(8,128)(2,1)} %get-tuple-element.16.y_ref) | copy-start | bytes 1966084

commit v2 on v0

--- a/solution.py
+++ b/solution.py
@@ -94,6 +94,619 @@
 def gather_rows(x, group, number):
     whole = exchange(x, *group, True, number)
     return whole.reshape((whole.shape[0] * whole.shape[1],) + whole.shape[2:])
+
+
+def rows_at(start, size):
+    return pl.ds(pl.multiple_of(start, 16), size)
+
+
+def cols_at(start, size):
+    return pl.ds(pl.multiple_of(start, 128), size)
+
+
+def partners(me, n):
+    if n == 2:
+        to = [1 - me]
+        return to, to
+    if n == 4:
+        near = me + 1 - 2 * lax.rem(me, 2)
+        to = [near, lax.rem(me + 2, 4), lax.rem(near + 2, 4)]
+        return to, to
+    return (
+        [lax.rem(me + k, n) for k in range(1, n)],
+        [lax.rem(me + n - k, n) for k in range(1, n)],
+    )
+
+
+class Plan:
+    def __init__(self, sizes, query, keys, resid, enc_weight):
+        self.grp, self.ctx, self.wid = sizes["grp"], sizes["ctx"], sizes["wid"]
+        self.high = self.wid // 2
+        self.shards = self.grp * self.ctx
+        self.row_count, self.heads_local, self.head_dim = query.shape
+        self.seqs, self.slots, self.kv_local = keys.shape[:3]
+        self.heads = self.heads_local // self.kv_local
+        self.width, self.latents = enc_weight.shape
+        self.cols = resid.shape[1]
+        self.streams = 2
+        self.rows = self.row_count // self.streams
+        self.half = self.rows // 2
+        self.quarter = self.rows // self.wid
+        self.side = self.rows // self.ctx
+        self.piece = self.side // self.grp
+        self.cuts = 5 if self.width % 640 == 0 else 2
+
+    def fits(self):
+        return (
+            self.wid % 2 == 0
+            and self.grp == self.wid == self.seqs
+            and self.ctx == self.kv_local
+            and self.ctx > 1
+            and self.rows % (16 * self.wid) == 0
+            and self.rows % (16 * self.shards) == 0
+            and self.cols % 128 == 0
+            and self.cols * self.ctx == self.width
+            and self.width % (128 * self.cuts) == 0
+            and self.latents % 512 == 0
+            and self.head_dim % 128 == 0
+            and self.heads % 2 == 0
+        )
+
+
+def fused_kernel(
+    plan, query, cache, key_pos, position, resid, enc_bias, dec_bias, out_hbm, enc_hbm, dec_hbm,
+    layer_out, block_t, lat_t, err, pgrad,
+    out_w, enc_w, dec_w, kv, att, proj, opair_in, opair_sum, ohigh_in, zin, block, lat,
+    part, pair_in, pair_sum, high_in, factor, recon, side_in, side_sum, piece_in,
+    load_sem, kv_sem, att_sem, att_cross, opair_sem, ohigh_sem, lo_sem, blk_sem, blk_cross,
+    pair_sem, high_sem, gather_sem, relay_sem, side_sem, piece_sem, spread_sem, cross_sem,
+):
+    p = plan
+    g, c, w = lax.axis_index("grp"), lax.axis_index("ctx"), lax.axis_index("wid")
+    low, high = lax.rem(w, 2), w // 2
+    partner = {"wid": w + 1 - 2 * low}
+    highs, highs_from = partners(high, p.high)
+    ctxs, ctxs_from = partners(c, p.ctx)
+    grps, grps_from = partners(g, p.grp)
+    to_high = lambda h: {"wid": h * 2 + low}
+    to_ctx = lambda q: {"ctx": q}
+    to_grp = lambda q: {"grp": q}
+    others = [(1 - low, high)] + [(low, h) for h in highs_from] + [(1 - low, h) for h in highs_from]
+    shard_to = [(q, r) for q in [g] + grps for r in [c] + ctxs][1:]
+    shard_from = [(q, r) for q in [g] + grps_from for r in [c] + ctxs_from][1:]
+
+    enc_step = 512
+    enc_steps = p.latents // enc_step
+
+    def load(src, dst, index):
+        copy = pltpu.make_async_copy(src, dst, load_sem.at[index])
+        copy.start()
+        return copy
+
+    barrier = pltpu.get_barrier_semaphore()
+    greeted = [{"grp": q, "ctx": r} for q, r in shard_to]
+    greeted += [{"wid": hi * 2 + lo} for lo, hi in others]
+    for peer in greeted:
+        pl.semaphore_signal(barrier, inc=1, device_id=peer, device_id_type=MESH)
+    out_load = load(out_hbm, out_w, 0)
+    enc_load = load(enc_hbm, enc_w, 1)
+    dec_load = load(dec_hbm, dec_w, 2)
+    pl.semaphore_wait(barrier, len(greeted))
+
+    pending = []
+
+    def send(src, dst, sem, index, peer, to_index=None, when=None):
+        copy = pltpu.make_async_remote_copy(
+            src_ref=src, dst_ref=dst, send_sem=sem.at[(0,) + index],
+            recv_sem=sem.at[(1,) + (index if to_index is None else to_index)],
+            device_id=peer, device_id_type=MESH,
+        )
+        if when is None:
+            copy.start()
+        else:
+            pl.when(when)(lambda: copy.start())
+        pending.append((copy, when))
+
+    def arrived(ref, sem, index):
+        pltpu.make_async_remote_copy(
+            src_ref=ref, dst_ref=ref, send_sem=sem.at[(0,) + index], recv_sem=sem.at[(1,) + index],
+            device_id=partner, device_id_type=MESH,
+        ).wait_recv()
+
+    def quarter_row(t, lo, hi):
+        return t * p.rows + (lo * p.high + hi) * p.quarter
+
+    def piece_row(t, q, r):
+        return t * p.rows + q * p.side + r * p.piece
+
+    def shard(q, r):
+        return q * p.ctx + r
+
+    def loop(count, body):
+        def step(i, carry):
+            body(pl.multiple_of(i * 16, 16))
+            return carry
+
+        lax.fori_loop(0, count // 16, step, 0)
+
+    def cache_send():
+        for k, (q, r) in reversed(list(enumerate(shard_to))):
+            send(
+                cache.at[shard(q, r)], kv.at[rows_at(shard(g, c) * p.slots, p.slots)],
+                kv_sem, (k,), {"grp": q, "ctx": r},
+            )
+        kv[rows_at(shard(g, c) * p.slots, p.slots)] = cache[shard(g, c)]
+
+    def cache_wait():
+        for k, (q, r) in enumerate(shard_from):
+            arrived(kv.at[rows_at(shard(q, r) * p.slots, p.slots)], kv_sem, (k,))
+
+    def att_at(t, q, r):
+        return att.at[
+            rows_at(quarter_row(t, lax.rem(q, 2), q // 2), p.quarter),
+            cols_at(r * p.heads * p.head_dim, p.heads * p.head_dim),
+        ]
+
+    def attend_rows(t):
+        two = 2 * p.quarter
+        visible = key_pos[...] <= position[t]
+        mine = att_at(t, g, c)
+        for i in range(p.heads // 2):
+            scores = lax.dot_general(
+                query[t, pl.ds(i * two, two)], kv[:, : p.head_dim], (((1,), (1,)), ((), ())),
+                preferred_element_type=jnp.float32,
+            ) * p.head_dim ** (-0.5)
+            peak = jnp.max(jnp.where(visible, scores, -1e30), axis=-1, keepdims=True)
+            weights = jnp.where(visible, jnp.exp(scores - peak), 0.0)
+            total = jnp.sum(weights, axis=-1, keepdims=True)
+            weighted = jnp.dot(
+                weights.astype(jnp.bfloat16), kv[:, p.head_dim :], preferred_element_type=jnp.float32
+            )
+            out = (weighted / total).astype(jnp.bfloat16)
+            for j in range(2):
+                mine[:, pl.ds((2 * i + j) * p.head_dim, p.head_dim)] = out[j * p.quarter : (j + 1) * p.quarter]
+        for k, q in enumerate(grps):
+            send(mine, mine, att_sem, (t, k), to_grp(q))
+        for i, r in enumerate(ctxs):
+            send(mine, mine, att_cross, (t, i, 0), to_ctx(r))
+
+    def att_relay(t):
+        for k, q in enumerate(grps_from):
+            theirs = att_at(t, q, c)
+            arrived(theirs, att_sem, (t, k))
+            for i, r in enumerate(ctxs):
+                send(theirs, theirs, att_cross, (t, i, k + 1), to_ctx(r))
+
+    def project(t):
+        for i, r in enumerate(ctxs_from):
+            for k, q in enumerate([g] + grps_from):
+                arrived(att_at(t, q, r), att_cross, (t, i, k))
+        if t == 0:
+            out_load.wait()
+        rows = pl.ds(t * p.rows, p.rows)
+        proj[rows] = jnp.dot(att[rows], out_w[...], preferred_element_type=jnp.float32).astype(jnp.bfloat16)
+        send(
+            proj.at[rows_at(t * p.rows + (1 - low) * p.half, p.half)], opair_in.at[t], opair_sem, (t,), partner
+        )
+
+    def project_add(t):
+        arrived(opair_in.at[t], opair_sem, (t,))
+
+        def body(r):
+            mine = proj[rows_at(t * p.rows + low * p.half + r, 16)].astype(jnp.float32)
+            opair_sum[t, pl.ds(r, 16)] = (mine + opair_in[t, pl.ds(r, 16)].astype(jnp.float32)).astype(jnp.bfloat16)
+
+        loop(p.half, body)
+        for s, h in enumerate(highs):
+            send(opair_sum.at[t, rows_at(h * p.quarter, p.quarter)], ohigh_in.at[t, s], ohigh_sem, (t, s), to_high(h))
+
+    def layer(t):
+        for s in range(len(highs)):
+            arrived(ohigh_in.at[t, s], ohigh_sem, (t, s))
+
+        def body(r):
+            total = opair_sum[t, rows_at(high * p.quarter + r, 16)].astype(jnp.float32)
+            for s in range(len(highs)):
+                total = total + ohigh_in[t, s, pl.ds(r, 16)].astype(jnp.float32)
+            rows = rows_at(t * p.quarter + r, 16)
+            value = (total + resid[rows].astype(jnp.float32)).astype(jnp.bfloat16)
+            layer_out[rows] = value
+            zin[t, g, pl.ds(r, 16)] = value
+
+        loop(p.quarter, body)
+        for k, q in enumerate(grps):
+            send(zin.at[t, g], zin.at[t, g], lo_sem, (t, k), to_grp(q))
+
+    def block_at(t, lo, hi, r):
+        return block.at[rows_at(quarter_row(t, lo, hi), p.quarter), cols_at(r * p.cols, p.cols)]
+
+    def block_relay(t):
+        mine = block_at(t, low, high, c)
+        for k, q in enumerate([g] + grps_from):
+            if k:
+                arrived(zin.at[t, q], lo_sem, (t, k - 1))
+            owned, away = w == q, w != q
+
+            @pl.when(owned)
+            def _(q=q):
+                mine[...] = zin[t, q]
+
+            for i, r in enumerate(ctxs):
+                send(mine, mine, blk_cross, (t, i, 0, k), to_ctx(r), (t, i, 0, 0), owned)
+            send(zin.at[t, q], mine, blk_sem, (t, k), {"wid": q}, (t, w), away)
+
+    def block_spread(t):
+        for j, (lo, hi) in enumerate(others):
+            theirs = block_at(t, lo, hi, c)
+            arrived(theirs, blk_sem, (t, hi * 2 + lo))
+            for i, r in enumerate(ctxs):
+                send(theirs, theirs, blk_cross, (t, i, j + 1, 0), to_ctx(r))
+
+    def block_wait(t):
+        for i, r in enumerate(ctxs_from):
+            for j, (lo, hi) in enumerate([(low, high)] + others):
+                arrived(block_at(t, lo, hi, r), blk_cross, (t, i, j, 0))
+
+    def pair_send(k, t):
+        there = part.at[k, rows_at(t * p.rows + (1 - low) * p.half, p.half)]
+        send(there, pair_in.at[k, t], pair_sem, (k, t), partner)
+
+    def pair_add(k, t):
+        arrived(pair_in.at[k, t], pair_sem, (k, t))
+
+        def body(r):
+            mine = part[k, rows_at(t * p.rows + low * p.half + r, 16)].astype(jnp.float32)
+            pair_sum[k, t, pl.ds(r, 16)] = (mine + pair_in[k, t, pl.ds(r, 16)].astype(jnp.float32)).astype(jnp.bfloat16)
+
+        loop(p.half, body)
+        for s, h in enumerate(highs):
+            send(pair_sum.at[k, t, rows_at(h * p.quarter, p.quarter)], high_in.at[k, t, s], high_sem, (k, t, s), to_high(h))
+
+    def high_sum(k, t, r):
+        total = pair_sum[k, t, rows_at(high * p.quarter + r, 16)].astype(jnp.float32)
+        for s in range(len(highs)):
+            total = total + high_in[k, t, s, pl.ds(r, 16)].astype(jnp.float32)
+        return total
+
+    def publish(k, t, out):
+        mine = out.at[rows_at(quarter_row(t, low, high), p.quarter)]
+        for s, h in enumerate(highs):
+            send(mine, mine, gather_sem, (k, t, s + 1), to_high(h))
+        send(mine, mine, gather_sem, (k, t, 0), partner)
+
+    def activate(t):
+        for s in range(len(highs)):
+            arrived(high_in.at[0, t, s], high_sem, (0, t, s))
+
+        def body(r):
+            z = 4.0 * (high_sum(0, t, r) + enc_bias[...])
+            e = jnp.exp(-jnp.abs(z))
+            lat[rows_at(quarter_row(t, low, high) + r, 16)] = (
+                (jnp.maximum(z, 0.0) + jnp.log1p(e)) * 0.25
+            ).astype(jnp.bfloat16)
+            factor[t, pl.ds(r, 16)] = jnp.where(z >= 0.0, 1.0, e) / (1.0 + e)
+
+        loop(p.quarter, body)
+        publish(0, t, lat)
+
+    def cotangent(t):
+        for s in range(len(highs)):
+            arrived(high_in.at[1, t, s], high_sem, (1, t, s))
+
+        def body(r):
+            pgrad[rows_at(quarter_row(t, low, high) + r, 16)] = (
+                high_sum(1, t, r) * factor[t, pl.ds(r, 16)]
+            ).astype(jnp.bfloat16)
+
+        loop(p.quarter, body)
+        publish(1, t, pgrad)
+
+    def relay(k, t, out):
+        for s, h in enumerate(highs_from):
+            theirs = out.at[rows_at(quarter_row(t, low, h), p.quarter)]
+            arrived(theirs, gather_sem, (k, t, s + 1))
+            send(theirs, theirs, relay_sem, (k, t, s), partner)
+
+    def collected(k, t, out):
+        arrived(out.at[rows_at(quarter_row(t, 1 - low, high), p.quarter)], gather_sem, (k, t, 0))
+        for s, h in enumerate(highs_from):
+            arrived(out.at[rows_at(quarter_row(t, 1 - low, h), p.quarter)], relay_sem, (k, t, s))
+
+    def encode(t):
+        block_wait(t)
+        if t == 0:
+            enc_load.wait()
+        rows = pl.ds(t * p.rows, p.rows)
+
+        def step(j, carry):
+            cols = cols_at(j * enc_step, enc_step)
+            part[0, rows, cols] = jnp.dot(
+                block[rows, :], enc_w[:, cols], preferred_element_type=jnp.float32
+            ).astype(jnp.bfloat16)
+            return carry
+
+        lax.fori_loop(0, enc_steps, step, 0)
+        pair_send(0, t)
+
+    cut = p.width // p.cuts
+
+    def decode(t):
+        collected(0, t, lat)
+        if t == 0:
+            dec_load.wait()
+        rows = pl.ds(t * p.rows, p.rows)
+        for j in range(p.cuts):
+            cols = pl.ds(j * cut, cut)
+            recon[rows, cols] = jnp.dot(
+                lat[rows, :], dec_w[:, cols], preferred_element_type=jnp.float32
+            ).astype(jnp.bfloat16)
+            for s, q in enumerate(ctxs):
+                send(
+                    recon.at[rows_at(piece_row(t, q, 0), p.side), cols], side_in.at[t, s, :, cols],
+                    side_sem, (t, j, s), to_ctx(q),
+                )
+
+    def side_add(t):
+        for j in range(p.cuts):
+            cols = pl.ds(j * cut, cut)
+            for s in range(len(ctxs)):
+                arrived(side_in.at[t, s, :, cols], side_sem, (t, j, s))
+            total = recon[rows_at(piece_row(t, c, 0), p.side), cols].astype(jnp.float32)
+            for s in range(len(ctxs)):
+                total = total + side_in[t, s, :, cols].astype(jnp.float32)
+            side_sum[t, :, cols] = total.astype(jnp.bfloat16)
+            for s, q in enumerate(grps):
+                send(
+                    side_sum.at[t, rows_at(q * p.piece, p.piece), cols], piece_in.at[t, s, :, cols],
+                    piece_sem, (t, j, s), to_grp(q),
+                )
+
+    def err_at(t, q, r, cols):
+        return err.at[rows_at(piece_row(t, q, r), p.piece), cols]
+
+    def error(t):
+        for j in range(p.cuts):
+            cols = pl.ds(j * cut, cut)
+            for s in range(len(grps)):
+                arrived(piece_in.at[t, s, :, cols], piece_sem, (t, j, s))
+            total = side_sum[t, rows_at(g * p.piece, p.piece), cols].astype(jnp.float32)
+            for s in range(len(grps)):
+                total = total + piece_in[t, s, :, cols].astype(jnp.float32)
+            rows = rows_at(piece_row(t, c, g), p.piece)
+            wanted = block[rows, cols].astype(jnp.float32)
+            err[rows, cols] = ((total + dec_bias[:, cols] - wanted) * p.row_count ** (-0.5)).astype(jnp.bfloat16)
+            mine = err_at(t, c, g, cols)
+            for s, q in enumerate(grps):
+                send(mine, mine, spread_sem, (t, j, s), to_grp(q))
+            for s, q in enumerate(ctxs):
+                send(mine, mine, cross_sem, (t, j, s, 0), to_ctx(q))
+
+    def error_relay(t):
+        for j in range(p.cuts):
+            cols = pl.ds(j * cut, cut)
+            for i, r in enumerate(grps_from):
+                theirs = err_at(t, c, r, cols)
+                arrived(theirs, spread_sem, (t, j, i))
+                for s, q in enumerate(ctxs):
+                    send(theirs, theirs, cross_sem, (t, j, s, i + 1), to_ctx(q))
+
+    def back(t):
+        for j in range(p.cuts):
+            for s, q in enumerate(ctxs_from):
+                for i, r in enumerate([g] + grps_from):
+                    arrived(err_at(t, q, r, pl.ds(j * cut, cut)), cross_sem, (t, j, s, i))
+        rows = pl.ds(t * p.rows, p.rows)
+
+        def step(j, carry):
+            cols = pl.ds(pl.multiple_of(j * enc_step, enc_step), enc_step)
+            part[1, rows, cols] = lax.dot_general(
+                err[rows, :], dec_w[cols, :], (((1,), (1,)), ((), ())), preferred_element_type=jnp.float32
+            ).astype(jnp.bfloat16)
+            return carry
+
+        lax.fori_loop(0, enc_steps, step, 0)
+        pair_send(1, t)
+
+    def turn(src, dst, t, count):
+        rows = pl.ds(t * p.rows, p.rows)
+
+        def step(j, carry):
+            cols = cols_at(j * 256, 256)
+            dst[cols, rows] = src[rows, cols].T
+            return carry
+
+        lax.fori_loop(0, count // 256, step, 0)
+
+    cache_send()
+    cache_wait()
+    stages = [
+        lambda: attend_rows(0),
+        lambda: attend_rows(1),
+        lambda: att_relay(0),
+        lambda: att_relay(1),
+        lambda: project(0),
+        lambda: project(1),
+        lambda: project_add(0),
+        lambda: project_add(1),
+        lambda: layer(0),
+        lambda: layer(1),
+        lambda: block_relay(0),
+        lambda: block_spread(0),
+        lambda: block_relay(1),
+        lambda: block_spread(1),
+        lambda: encode(0),
+        lambda: encode(1),
+        lambda: pair_add(0, 0),
+        lambda: pair_add(0, 1),
+        lambda: turn(block, block_t, 0, p.width),
+        lambda: turn(block, block_t, 1, p.width),
+        lambda: activate(0),
+        lambda: activate(1),
+        lambda: relay(0, 0, lat),
+        lambda: decode(0),
+        lambda: turn(lat, lat_t, 0, p.latents),
+        lambda: relay(0, 1, lat),
+        lambda: side_add(0),
+        lambda: decode(1),
+        lambda: error(0),
+        lambda: side_add(1),
+        lambda: turn(lat, lat_t, 1, p.latents),
+        lambda: error_relay(0),
+        lambda: error(1),
+        lambda: back(0),
+        lambda: error_relay(1),
+        lambda: pair_add(1, 0),
+        lambda: back(1),
+        lambda: pair_add(1, 1),
+        lambda: cotangent(0),
+        lambda: cotangent(1),
+        lambda: relay(1, 0, pgrad),
+        lambda: relay(1, 1, pgrad),
+        lambda: collected(1, 0, pgrad),
+        lambda: collected(1, 1, pgrad),
+    ]
+    for stage in stages:
+        stage()
+    for copy, when in pending:
+        if when is None:
+            copy.wait_send()
+        else:
+            pl.when(when)(lambda copy=copy: copy.wait_send())
+
+
+def fused(plan, query, keys, values, lengths, query_pos, resid, out_weight, enc_weight, enc_bias, dec_weight, dec_bias):
+    p = plan
+    low = jnp.bfloat16
+    g, c = lax.axis_index("grp"), lax.axis_index("ctx")
+    cache = jnp.concatenate([keys, values], axis=-1).transpose(0, 2, 1, 3)
+    cache = cache.reshape(p.shards, p.slots, 2 * p.head_dim)
+    seq_rows = p.row_count // p.seqs
+    mine = lax.dynamic_slice(query, (g * seq_rows, c * p.heads, 0), (seq_rows, p.heads, p.head_dim))
+    mine = mine.reshape(p.streams, p.quarter, p.heads, p.head_dim).transpose(0, 2, 1, 3)
+    mine = mine.reshape(p.streams, p.heads * p.quarter, p.head_dim)
+    live = lax.dynamic_index_in_dim(lengths, g, 0, keepdims=False)
+    before = jnp.arange(p.shards)[None, :] < jnp.arange(p.shards)[:, None]
+    offset = jnp.sum(jnp.where(before, live[None, :], 0), axis=1)
+    slot_ids = jnp.arange(p.slots, dtype=jnp.int32)
+    key_pos = jnp.where(
+        slot_ids[None, :] < live[:, None], offset[:, None] + slot_ids[None, :], jnp.int32(2**30)
+    ).reshape(1, -1)
+    position = lax.dynamic_slice_in_dim(query_pos, g * seq_rows, seq_rows, 0).reshape(p.streams, 1, p.quarter)
+    position = jnp.broadcast_to(position, (p.streams, 2, p.quarter)).reshape(p.streams, 2 * p.quarter, 1)
+
+    vmem = pl.BlockSpec(memory_space=pltpu.VMEM)
+    hbm = pl.BlockSpec(memory_space=pltpu.HBM)
+    n, highs, ctxs, grps = p.streams, p.high - 1, p.ctx - 1, p.grp - 1
+    dma = pltpu.SemaphoreType.DMA
+    return pl.pallas_call(
+        functools.partial(fused_kernel, p),
+        out_shape=(
+            jax.ShapeDtypeStruct((n * p.quarter, p.cols), low),
+            jax.ShapeDtypeStruct((p.width, p.row_count), low),
+            jax.ShapeDtypeStruct((p.latents, p.row_count), low),
+            jax.ShapeDtypeStruct((p.row_count, p.width), low),
+            jax.ShapeDtypeStruct((p.row_count, p.latents), low),
+        ),
+        in_specs=[vmem] * 7 + [hbm] * 3,
+        out_specs=(vmem,) * 5,
+        scratch_shapes=[
+            pltpu.VMEM(out_weight.shape, low),
+            pltpu.VMEM((p.width, p.latents), low),
+            pltpu.VMEM((p.latents, p.width), low),
+            pltpu.VMEM((p.shards * p.slots, 2 * p.head_dim), low),
+            pltpu.VMEM((p.row_count, p.heads_local * p.head_dim), low),
+            pltpu.VMEM((p.row_count, p.cols), low),
+            pltpu.VMEM((n, p.half, p.cols), low),
+            pltpu.VMEM((n, p.half, p.cols), low),
+            pltpu.VMEM((n, highs, p.quarter, p.cols), low),
+            pltpu.VMEM((n, p.grp, p.quarter, p.cols), low),
+            pltpu.VMEM((p.row_count, p.width), low),
+            pltpu.VMEM((p.row_count, p.latents), low),
+            pltpu.VMEM((2, p.row_count, p.latents), low),
+            pltpu.VMEM((2, n, p.half, p.latents), low),
+            pltpu.VMEM((2, n, p.half, p.latents), low),
+            pltpu.VMEM((2, n, highs, p.quarter, p.latents), low),
+            pltpu.VMEM((n, p.quarter, p.latents), jnp.float32),
+            pltpu.VMEM((p.row_count, p.width), low),
+            pltpu.VMEM((n, ctxs, p.side, p.width), low),
+            pltpu.VMEM((n, p.side, p.width), low),
+            pltpu.VMEM((n, grps, p.piece, p.width), low),
+            dma((3,)),
+            dma((2, p.shards - 1)),
+            dma((2, n, grps)),
+            dma((2, n, ctxs, grps + 1)),
+            dma((2, n)),
+            dma((2, n, highs)),
+            dma((2, n, grps)),
+            dma((2, n, p.grp)),
+            dma((2, n, ctxs, p.wid, p.grp)),
+            dma((2, 2, n)),
+            dma((2, 2, n, highs)),
+            dma((2, 2, n, highs + 1)),
+            dma((2, 2, n, highs)),
+            dma((2, n, p.cuts, ctxs)),
+            dma((2, n, p.cuts, grps)),
+            dma((2, n, p.cuts, grps)),
+            dma((2, n, p.cuts, ctxs, grps + 1)),
+        ],
+        compiler_params=pltpu.CompilerParams(
+            collective_id=0, has_side_effects=True, vmem_limit_bytes=44 * 1024 * 1024
+        ),
+        name="fused",
+    )(
+        mine, cache, key_pos, position, resid, enc_bias.reshape(1, -1), dec_bias.reshape(1, -1),
+        out_weight, enc_weight, dec_weight,
+    )
+
+
+def grads_kernel(dec_step, enc_step, depth, block_t, lat_t, err, pgrad, layer_in, enc_out, dec_out, enc_sum, dec_sum, layer_out, dec_buf, enc_buf, sem):
+    layer_out[...] = layer_in[...]
+    jobs = [(0, i) for i in range(dec_out.shape[0] // dec_step)]
+    jobs += [(1, i) for i in range(enc_out.shape[0] // enc_step)]
+    started = []
+    for k, (kind, i) in enumerate(jobs):
+        x, y, out, buf, step = ((lat_t, err, dec_out, dec_buf, dec_step), (block_t, pgrad, enc_out, enc_buf, enc_step))[kind]
+        slot = i % depth
+        if i >= depth:
+            started[k - depth].wait()
+        rows = pl.ds(i * step, step)
+        buf[slot] = jnp.dot(x[rows, :], y[...], preferred_element_type=jnp.float32).astype(jnp.bfloat16)
+        copy = pltpu.make_async_copy(buf.at[slot], out.at[rows], sem.at[kind, slot])
+        copy.start()
+        started.append(copy)
+    dec_sum[...] = jnp.sum(err[...].astype(jnp.float32), axis=0, keepdims=True)
+    enc_sum[...] = jnp.sum(pgrad[...].astype(jnp.float32), axis=0, keepdims=True)
+    for k, (kind, i) in enumerate(jobs):
+        count = sum(1 for job in jobs if job[0] == kind)
+        if i >= count - depth:
+            started[k].wait()
+
+
+def grads(block_t, lat_t, err, pgrad, layer_in):
+    width, latents = block_t.shape[0], lat_t.shape[0]
+    vmem = pl.BlockSpec(memory_space=pltpu.VMEM)
+    hbm = pl.BlockSpec(memory_space=pltpu.HBM)
+    dec_step, enc_step, depth = 256, 128, 4
+    enc, dec, enc_sum, dec_sum, layer_out = pl.pallas_call(
+        functools.partial(grads_kernel, dec_step, enc_step, depth),
+        out_shape=(
+            jax.ShapeDtypeStruct((width, latents), jnp.bfloat16),
+            jax.ShapeDtypeStruct((latents, width), jnp.bfloat16),
+            jax.ShapeDtypeStruct((1, latents), jnp.float32),
+            jax.ShapeDtypeStruct((1, width), jnp.float32),
+            jax.ShapeDtypeStruct(layer_in.shape, layer_in.dtype),
+        ),
+        in_specs=[vmem] * 5,
+        out_specs=(hbm, hbm, vmem, vmem, vmem),
+        scratch_shapes=[
+            pltpu.VMEM((depth, dec_step, width), jnp.bfloat16),
+            pltpu.VMEM((depth, enc_step, latents), jnp.bfloat16),
+            pltpu.SemaphoreType.DMA((2, depth)),
+        ],
+        compiler_params=pltpu.CompilerParams(vmem_limit_bytes=16 * 1024 * 1024),
+        name="grads",
+    )(block_t, lat_t, err, pgrad, layer_in)
+    return layer_out, enc, enc_sum.reshape(-1), dec, dec_sum.reshape(-1)
 
 
 def attend(groups, query, keys, values, lengths, query_pos):
@@ -152,6 +765,13 @@
     dec_weight,
     dec_bias,
 ):
+    plan = Plan(sizes, query, keys, resid, enc_weight)
+    if plan.fits():
+        layer_out, block_t, lat_t, err, pgrad = fused(
+            plan, query, keys, values, lengths, query_pos, resid, out_weight,
+            enc_weight, enc_bias, dec_weight, dec_bias,
+        )
+        return grads(block_t, lat_t, err, pgrad, layer_out)
     groups = Groups(sizes)
     row_count = query.shape[0]
     shard_pos = lax.axis_index(("grp", "ctx"))

time: 217 us -> 134 us (0.62)
  Pallas kernels: 158 us -> 125 us
  matrix products: 31.8 us -> 0 us
  other arithmetic: 12.1 us -> 2.06 us
  local copies, waits for them, and re-layouts: 11.3 us -> 5.91 us
    pallas_call x15 -> x2, Pallas kernels: 158 us -> 125 us  [the longest x1 115 us: fused(): pl.pallas_call(functools.partial(fused_kernel, p), out_shape=(jax.ShapeDt...]
    dot_general x8 -> x0, matrix products: 31.8 us -> none  [the longest x1 5.99 us: body(): recon = jnp.dot(latents, dec_weight, preferred_element_type=jnp.float32)]
    reduce_sum x9 -> x1, other arithmetic: 7.68 us -> 0.12 us  [fused(): offset = jnp.sum(jnp.where(before, live[None, :], 0), axis=1)]
    unnamed x36 -> x8, local copies, waits for them, and re-layouts: 7.41 us -> 3.34 us
    reshape x3 -> x2, local copies, waits for them, and re-layouts: 3.01 us -> 0.8 us  [the longest x1 0.7 us: fused(): dec_bias.reshape(1, -1)]
where the time goes in v2:
time: 134 us
  Pallas kernels  125 us (93%)
  local copies, waits for them, and re-layouts  5.91 us (4%)
  other arithmetic  2.06 us (2%)
    pallas_call x1, Pallas kernels, fused(): pl.pallas_call(functools.partial(fused_kernel, p), out_shape=(jax.ShapeDt...  115 us
    pallas_call x1, Pallas kernels, grads(): pl.pallas_call(functools.partial(grads_kernel, dec_step, enc_step, depth)...  9.62 us
    unnamed x8, local copies, waits for them, and re-layouts  3.34 us

profile of v2, /device:TPU:0, one launch (start us, length us, event | category | flops | bytes accessed | tf_op | source)
XLA Modules:
  0.0 133.6 jit_solution(8748117279947718267)
XLA Ops:
  0.6 0.0 copy-start
  0.7 0.8 dynamic-slice_bitcast_fusion
  1.4 0.1 select_reduce_fusion
  1.5 0.8 dynamic_slice.12
  2.3 0.1 broadcast_in_dim.33
  2.4 0.1 add_select_fusion
  2.5 0.1 select_n.34.key_pos
  2.5 0.7 reshape.94.dec_bias
  3.2 0.1 reshape.97.position
  3.4 0.0 copy-done
  3.4 1.2 maximum_bitcast_fusion
  4.7 0.0 copy-start.1
  4.7 1.7 %copy-done.1 = bf16[2048,640]{1,0:T(8,128)(2,1)S(1)} copy-done((bf16[2048,640]{1,0:T(8,128)(2,1)S(1)}, bf16[2048,640]{1,0:T(8,128)(2,1)}, u32[]{:S(2)}) %copy-start.1) | copy-done | bytes 2621464
  6.5 0.0 copy-start.2
  6.5 0.9 copy-done.2
  7.3 0.0 copy-start.3
  7.3 0.7 copy-done.3
  8.0 115.3 %fused.1 = (bf16[64,640]{1,0:T(8,128)(2,1)S(1)}, bf16[1280,256]{1,0:T(8,128)(2,1)S(1)}, bf16[3072,256]{1,0:T(8,128)(2,1)S(1)}, bf16[256,1280]{1,0:T(8,128)(2,1)S(1)}, bf16[256,3072]{1,0:T(8,128)(2,1)S(1)}) custom-call(bf16[2,256,128]{2,1,0:T(8,128)(2,1)S(1)} %bitcast.12, bf16[8,64,256]{2,1,0:T(8,128)(2,1)S(1)} %bitcast.11, s32[1,512]{1,0:T(1,128)S(1)} %select_n.34.key_pos, ...), custom_call_target="tpu_custom_call" | custom-call | tf_op jit(solution)/shard_map/fused/pallas_call | solution.py:601
  123.3 9.6 %grads.1 = (bf16[1280,3072]{1,0:T(8,128)(2,1)}, bf16[3072,1280]{1,0:T(8,128)(2,1)}, f32[1,3072]{1,0:T(1,128)}, f32[1,1280]{1,0:T(1,128)S(1)}, bf16[64,640]{1,0:T(8,128)(2,1)}) custom-call(bf16[1280,256]{1,0:T(8,128)(2,1)S(1)} %get-tuple-element.15.block_t, bf16[3072,256]{1,0:T(8,128)(2,1)S(1)} %get-tuple-element.16.lat_t, ...), custom_call_target="tpu_custom_call" | custom-call | tf_op jit(solution)/shard_map/grads/pallas_call | solution.py:690
  133.0 0.6 reduce
  (4 shorter events, 0.1 us)
Async XLA Ops:
  0.6 2.7 %copy-start = (bf16[256,16,128]{2,1,0:T(8,128)(2,1)S(1)}, bf16[256,16,128]{2,1,0:T(8,128)(2,1)}, u32[]{:S(2)}) copy-start(bf16[256,16,128]{2,1,0:T(8,128)(2,1)} %param.11) | copy-start | bytes 3145732
  4.7 1.7 %copy-start.1 = (bf16[2048,640]{1,0:T(8,128)(2,1)S(1)}, bf16[2048,640]{1,0:T(8,128)(2,1)}, u32[]{:S(2)}) copy-start(bf16[2048,640]{1,0:T(8,128)(2,1)} %out_hbm.1) | copy-start | bytes 7864324
  6.5 0.9 copy-start.2
  7.3 0.7 copy-start.3

commit v3 on v2

--- a/solution.py
+++ b/solution.py
@@ -154,9 +154,9 @@
 
 
 def fused_kernel(
-    plan, query, cache, key_pos, position, resid, enc_bias, dec_bias, out_hbm, enc_hbm, dec_hbm,
+    plan, query, cache, len_hbm, pos_hbm, resid_hbm, eb_hbm, db_hbm, out_hbm, enc_hbm, dec_hbm,
     layer_out, block_t, lat_t, err, pgrad,
-    out_w, enc_w, dec_w, kv, att, proj, opair_in, opair_sum, ohigh_in, zin, block, lat,
+    lengths, query_pos, resid, enc_bias, dec_bias, out_w, enc_w, dec_w, kv, att, proj, opair_in, opair_sum, ohigh_in, zin, block, lat,
     part, pair_in, pair_sum, high_in, factor, recon, side_in, side_sum, piece_in,
     load_sem, kv_sem, att_sem, att_cross, opair_sem, ohigh_sem, lo_sem, blk_sem, blk_cross,
     pair_sem, high_sem, gather_sem, relay_sem, side_sem, piece_sem, spread_sem, cross_sem,
@@ -188,6 +188,12 @@
     greeted += [{"wid": hi * 2 + lo} for lo, hi in others]
     for peer in greeted:
         pl.semaphore_signal(barrier, inc=1, device_id=peer, device_id_type=MESH)
+    small_loads = [
+        load(src, dst, 3 + k)
+        for k, (src, dst) in enumerate(
+            [(len_hbm, lengths), (pos_hbm, query_pos), (resid_hbm, resid), (eb_hbm, enc_bias), (db_hbm, dec_bias)]
+        )
+    ]
     out_load = load(out_hbm, out_w, 0)
     enc_load = load(enc_hbm, enc_w, 1)
     dec_load = load(dec_hbm, dec_w, 2)
@@ -247,9 +253,29 @@
             cols_at(r * p.heads * p.head_dim, p.heads * p.head_dim),
         ]
 
+    def key_positions():
+        live = lengths[pl.ds(g, 1), :]
+        slot = lax.broadcasted_iota(jnp.int32, (1, p.shards * p.slots), 1)
+        key = jnp.full((1, p.shards * p.slots), 2**30, jnp.int32)
+        offset = jnp.zeros((1, 1), jnp.int32)
+        for b in range(p.shards):
+            count = live[:, b : b + 1]
+            own = slot - b * p.slots
+            key = jnp.where((own >= 0) & (own < p.slots) & (own < count), offset + own, key)
+            offset = offset + count
+        return key
+
+    def row_positions(t):
+        shape = (2 * p.quarter, p.row_count)
+        row = lax.broadcasted_iota(jnp.int32, shape, 0)
+        wanted = lax.rem(row, p.quarter) + (g * (p.row_count // p.seqs) + t * p.quarter)
+        here = lax.broadcasted_iota(jnp.int32, shape, 1) == wanted
+        values = jnp.where(here, query_pos[...].reshape(1, -1).astype(jnp.float32), 0.0)
+        return jnp.sum(values, axis=1, keepdims=True).astype(jnp.int32)
+
     def attend_rows(t):
         two = 2 * p.quarter
-        visible = key_pos[...] <= position[t]
+        visible = key_positions() <= row_positions(t)
         mine = att_at(t, g, c)
         for i in range(p.heads // 2):
             scores = lax.dot_general(
@@ -379,7 +405,7 @@
             arrived(high_in.at[0, t, s], high_sem, (0, t, s))
 
         def body(r):
-            z = 4.0 * (high_sum(0, t, r) + enc_bias[...])
+            z = 4.0 * (high_sum(0, t, r) + enc_bias[...].reshape(1, -1))
             e = jnp.exp(-jnp.abs(z))
             lat[rows_at(quarter_row(t, low, high) + r, 16)] = (
                 (jnp.maximum(z, 0.0) + jnp.log1p(e)) * 0.25
@@ -474,7 +500,7 @@
                 total = total + piece_in[t, s, :, cols].astype(jnp.float32)
             rows = rows_at(piece_row(t, c, g), p.piece)
             wanted = block[rows, cols].astype(jnp.float32)
-            err[rows, cols] = ((total + dec_bias[:, cols] - wanted) * p.row_count ** (-0.5)).astype(jnp.bfloat16)
+            err[rows, cols] = ((total + dec_bias[cols].reshape(1, -1) - wanted) * p.row_count ** (-0.5)).astype(jnp.bfloat16)
             mine = err_at(t, c, g, cols)
             for s, q in enumerate(grps):
                 send(mine, mine, spread_sem, (t, j, s), to_grp(q))
@@ -518,25 +544,27 @@
         lax.fori_loop(0, count // 256, step, 0)
 
     cache_send()
+    for copy in small_loads:
+        copy.wait()
     cache_wait()
     stages = [
         lambda: attend_rows(0),
         lambda: attend_rows(1),
         lambda: att_relay(0),
+        lambda: project(0),
         lambda: att_relay(1),
-        lambda: project(0),
+        lambda: project_add(0),
         lambda: project(1),
-        lambda: project_add(0),
+        lambda: layer(0),
         lambda: project_add(1),
-        lambda: layer(0),
+        lambda: block_relay(0),
         lambda: layer(1),
-        lambda: block_relay(0),
         lambda: block_spread(0),
         lambda: block_relay(1),
         lambda: block_spread(1),
         lambda: encode(0),
+        lambda: pair_add(0, 0),
         lambda: encode(1),
-        lambda: pair_add(0, 0),
         lambda: pair_add(0, 1),
         lambda: turn(block, block_t, 0, p.width),
         lambda: turn(block, block_t, 1, p.width),
@@ -584,15 +612,6 @@
     mine = lax.dynamic_slice(query, (g * seq_rows, c * p.heads, 0), (seq_rows, p.heads, p.head_dim))
     mine = mine.reshape(p.streams, p.quarter, p.heads, p.head_dim).transpose(0, 2, 1, 3)
     mine = mine.reshape(p.streams, p.heads * p.quarter, p.head_dim)
-    live = lax.dynamic_index_in_dim(lengths, g, 0, keepdims=False)
-    before = jnp.arange(p.shards)[None, :] < jnp.arange(p.shards)[:, None]
-    offset = jnp.sum(jnp.where(before, live[None, :], 0), axis=1)
-    slot_ids = jnp.arange(p.slots, dtype=jnp.int32)
-    key_pos = jnp.where(
-        slot_ids[None, :] < live[:, None], offset[:, None] + slot_ids[None, :], jnp.int32(2**30)
-    ).reshape(1, -1)
-    position = lax.dynamic_slice_in_dim(query_pos, g * seq_rows, seq_rows, 0).reshape(p.streams, 1, p.quarter)
-    position = jnp.broadcast_to(position, (p.streams, 2, p.quarter)).reshape(p.streams, 2 * p.quarter, 1)
 
     vmem = pl.BlockSpec(memory_space=pltpu.VMEM)
     hbm = pl.BlockSpec(memory_space=pltpu.HBM)
@@ -607,9 +626,14 @@
             jax.ShapeDtypeStruct((p.row_count, p.width), low),
             jax.ShapeDtypeStruct((p.row_count, p.latents), low),
         ),
-        in_specs=[vmem] * 7 + [hbm] * 3,
+        in_specs=[vmem] * 2 + [hbm] * 8,
         out_specs=(vmem,) * 5,
         scratch_shapes=[
+            pltpu.VMEM(lengths.shape, jnp.int32),
+            pltpu.VMEM(query_pos.shape, jnp.int32),
+            pltpu.VMEM(resid.shape, low),
+            pltpu.VMEM(enc_bias.shape, jnp.float32),
+            pltpu.VMEM(dec_bias.shape, jnp.float32),
             pltpu.VMEM(out_weight.shape, low),
             pltpu.VMEM((p.width, p.latents), low),
             pltpu.VMEM((p.latents, p.width), low),
@@ -631,7 +655,7 @@
             pltpu.VMEM((n, ctxs, p.side, p.width), low),
             pltpu.VMEM((n, p.side, p.width), low),
             pltpu.VMEM((n, grps, p.piece, p.width), low),
-            dma((3,)),
+            dma((8,)),
             dma((2, p.shards - 1)),
             dma((2, n, grps)),
             dma((2, n, ctxs, grps + 1)),
@@ -654,8 +678,11 @@
         ),
         name="fused",
     )(
-        mine, cache, key_pos, position, resid, enc_bias.reshape(1, -1), dec_bias.reshape(1, -1),
-        out_weight, enc_weight, dec_weight,
+        mine, cache,
+        *(
+            pltpu.with_memory_space_constraint(x, pltpu.HBM)
+            for x in (lengths, query_pos, resid, enc_bias, dec_bias, out_weight, enc_weight, dec_weight)
+        ),
     )
 
 
@@ -674,8 +701,8 @@
         copy = pltpu.make_async_copy(buf.at[slot], out.at[rows], sem.at[kind, slot])
         copy.start()
         started.append(copy)
-    dec_sum[...] = jnp.sum(err[...].astype(jnp.float32), axis=0, keepdims=True)
-    enc_sum[...] = jnp.sum(pgrad[...].astype(jnp.float32), axis=0, keepdims=True)
+    dec_sum[...] = jnp.sum(err[...].astype(jnp.float32), axis=0)
+    enc_sum[...] = jnp.sum(pgrad[...].astype(jnp.float32), axis=0)
     for k, (kind, i) in enumerate(jobs):
         count = sum(1 for job in jobs if job[0] == kind)
         if i >= count - depth:
@@ -686,14 +713,14 @@
     width, latents = block_t.shape[0], lat_t.shape[0]
     vmem = pl.BlockSpec(memory_space=pltpu.VMEM)
     hbm = pl.BlockSpec(memory_space=pltpu.HBM)
-    dec_step, enc_step, depth = 256, 128, 4
+    dec_step, enc_step, depth = 1024, 256, 3
     enc, dec, enc_sum, dec_sum, layer_out = pl.pallas_call(
         functools.partial(grads_kernel, dec_step, enc_step, depth),
         out_shape=(
             jax.ShapeDtypeStruct((width, latents), jnp.bfloat16),
             jax.ShapeDtypeStruct((latents, width), jnp.bfloat16),
-            jax.ShapeDtypeStruct((1, latents), jnp.float32),
-            jax.ShapeDtypeStruct((1, width), jnp.float32),
+            jax.ShapeDtypeStruct((latents,), jnp.float32),
+            jax.ShapeDtypeStruct((width,), jnp.float32),
             jax.ShapeDtypeStruct(layer_in.shape, layer_in.dtype),
         ),
         in_specs=[vmem] * 5,
@@ -703,10 +730,10 @@
             pltpu.VMEM((depth, enc_step, latents), jnp.bfloat16),
             pltpu.SemaphoreType.DMA((2, depth)),
         ],
-        compiler_params=pltpu.CompilerParams(vmem_limit_bytes=16 * 1024 * 1024),
+        compiler_params=pltpu.CompilerParams(vmem_limit_bytes=24 * 1024 * 1024),
         name="grads",
     )(block_t, lat_t, err, pgrad, layer_in)
-    return layer_out, enc, enc_sum.reshape(-1), dec, dec_sum.reshape(-1)
+    return layer_out, enc, enc_sum, dec, dec_sum
 
 
 def attend(groups, query, keys, values, lengths, query_pos):

time: 134 us -> 125 us (0.933)
  local copies, waits for them, and re-layouts: 5.91 us -> 1.28 us
  Pallas kernels: 125 us -> 121 us
    pallas_call x1, Pallas kernels: 115 us -> 113 us  [fused(): pl.pallas_call(functools.partial(fused_kernel, p), out_shape=(jax.ShapeDt...]
    unnamed x8 -> x2, local copies, waits for them, and re-layouts: 3.34 us -> 1.22 us
    pallas_call x1, Pallas kernels: 9.62 us -> 8.06 us  [grads(): pl.pallas_call(functools.partial(grads_kernel, dec_step, enc_step, depth)...]
where the time goes in v3:
time: 125 us; the launch traced here: 124 us
  Pallas kernels  121 us (97%)
  local copies, waits for them, and re-layouts  1.28 us (1%)
  other arithmetic  1.25 us (1%)
    pallas_call x1, Pallas kernels, fused(): pl.pallas_call(functools.partial(fused_kernel, p), out_shape=(jax.ShapeDt...  113 us
    pallas_call x1, Pallas kernels, grads(): pl.pallas_call(functools.partial(grads_kernel, dec_step, enc_step, depth)...  8.06 us

profile of v3, /device:TPU:0, one launch (start us, length us, event | category | flops | bytes accessed | tf_op | source)
XLA Modules:
  0.0 124.4 jit_solution(3391170557850891444)
XLA Ops:
  0.6 0.0 copy-start
  0.7 1.2 copy-done
  1.9 1.2 %maximum_bitcast_fusion = bf16[4,2,64,256]{3,1,2,0:T(2,128)(2,1)S(1)} fusion(bf16[4,64,2,128]{3,2,1,0:T(2,128)(2,1)} %param.13, bf16[4,64,2,128]{3,2,1,0:T(2,128)(2,1)} %param.12), kind=kLoop, calls=%fused_computation | loop fusion | flops 524288 | bytes 524288 | tf_op jit(solution)/shard_map/transpose | solution.py:609
  3.2 112.9 %fused.1 = (bf16[64,640]{1,0:T(8,128)(2,1)S(1)}, bf16[1280,256]{1,0:T(8,128)(2,1)S(1)}, bf16[3072,256]{1,0:T(8,128)(2,1)S(1)}, bf16[256,1280]{1,0:T(8,128)(2,1)S(1)}, bf16[256,3072]{1,0:T(8,128)(2,1)S(1)}) custom-call(bf16[2,256,128]{2,1,0:T(8,128)(2,1)S(1)} %bitcast.8, bf16[8,64,256]{2,1,0:T(8,128)(2,1)S(1)} %bitcast.7, s32[4,8]{1,0:T(4,128)} %len_hbm.1, ...), custom_call_target="tpu_custom_call" | custom-call | tf_op jit(solution)/shard_map/fused/pallas_call | solution.py:620
  116.1 8.1 %grads.1 = (bf16[1280,3072]{1,0:T(8,128)(2,1)}, bf16[3072,1280]{1,0:T(8,128)(2,1)}, f32[3072]{0:T(1024)}, f32[1280]{0:T(1024)}, bf16[64,640]{1,0:T(8,128)(2,1)}) custom-call(bf16[1280,256]{1,0:T(8,128)(2,1)S(1)} %get-tuple-element.15.block_t, bf16[3072,256]{1,0:T(8,128)(2,1)S(1)} %get-tuple-element.16.lat_t, bf16[256,1280]{1,0:T(8,128)(2,1)S(1)} %get-tuple-element.17.err, ...), custom_call_target="tpu_custom_call" | custom-call | tf_op jit(solution)/shard_map/grads/pallas_call | solution.py:717
  (3 shorter events, 0.1 us)
Async XLA Ops:
  0.6 1.2 copy-start

commit v4 on v3

--- a/solution.py
+++ b/solution.py
@@ -134,7 +134,7 @@
         self.quarter = self.rows // self.wid
         self.side = self.rows // self.ctx
         self.piece = self.side // self.grp
-        self.cuts = 5 if self.width % 640 == 0 else 2
+        self.cuts = 2
 
     def fits(self):
         return (
@@ -155,8 +155,8 @@
 
 def fused_kernel(
     plan, query, cache, len_hbm, pos_hbm, resid_hbm, eb_hbm, db_hbm, out_hbm, enc_hbm, dec_hbm,
-    layer_out, block_t, lat_t, err, pgrad,
-    lengths, query_pos, resid, enc_bias, dec_bias, out_w, enc_w, dec_w, kv, att, proj, opair_in, opair_sum, ohigh_in, zin, block, lat,
+    layer_out, block_t, dec_grad, dec_sum, pgrad,
+    lat_t, err, lengths, query_pos, resid, enc_bias, dec_bias, out_w, enc_w, dec_w, kv, att, proj, opair_in, opair_sum, ohigh_in, zin, block, lat,
     part, pair_in, pair_sum, high_in, factor, recon, side_in, side_sum, piece_in,
     load_sem, kv_sem, att_sem, att_cross, opair_sem, ohigh_sem, lo_sem, blk_sem, blk_cross,
     pair_sem, high_sem, gather_sem, relay_sem, side_sem, piece_sem, spread_sem, cross_sem,
@@ -532,6 +532,19 @@
 
         lax.fori_loop(0, enc_steps, step, 0)
         pair_send(1, t)
+
+    out_step = 512
+
+    def outer(j):
+        rows = pl.ds(j * out_step, out_step)
+        dec_grad[rows] = jnp.dot(lat_t[rows, :], err[...], preferred_element_type=jnp.float32).astype(jnp.bfloat16)
+
+    def error_sum():
+        dec_sum[...] = jnp.sum(err[...].astype(jnp.float32), axis=0)
+
+    def outers(first, last):
+        for j in range(first * (p.latents // out_step) // 6, last * (p.latents // out_step) // 6):
+            outer(j)
 
     def turn(src, dst, t, count):
         rows = pl.ds(t * p.rows, p.rows)
@@ -587,7 +600,10 @@
         lambda: back(1),
         lambda: pair_add(1, 1),
         lambda: cotangent(0),
+        lambda: outers(0, 3),
         lambda: cotangent(1),
+        lambda: outers(3, 6),
+        error_sum,
         lambda: relay(1, 0, pgrad),
         lambda: relay(1, 1, pgrad),
         lambda: collected(1, 0, pgrad),
@@ -622,13 +638,15 @@
         out_shape=(
             jax.ShapeDtypeStruct((n * p.quarter, p.cols), low),
             jax.ShapeDtypeStruct((p.width, p.row_count), low),
-            jax.ShapeDtypeStruct((p.latents, p.row_count), low),
-            jax.ShapeDtypeStruct((p.row_count, p.width), low),
+            jax.ShapeDtypeStruct((p.latents, p.width), low),
+            jax.ShapeDtypeStruct((p.width,), jnp.float32),
             jax.ShapeDtypeStruct((p.row_count, p.latents), low),
         ),
         in_specs=[vmem] * 2 + [hbm] * 8,
         out_specs=(vmem,) * 5,
         scratch_shapes=[
+            pltpu.VMEM((p.latents, p.row_count), low),
+            pltpu.VMEM((p.row_count, p.width), low),
             pltpu.VMEM(lengths.shape, jnp.int32),
             pltpu.VMEM(query_pos.shape, jnp.int32),
             pltpu.VMEM(resid.shape, low),
@@ -674,7 +692,7 @@
             dma((2, n, p.cuts, ctxs, grps + 1)),
         ],
         compiler_params=pltpu.CompilerParams(
-            collective_id=0, has_side_effects=True, vmem_limit_bytes=44 * 1024 * 1024
+            collective_id=0, has_side_effects=True, vmem_limit_bytes=40 * 1024 * 1024
         ),
         name="fused",
     )(
@@ -686,36 +704,43 @@
     )
 
 
-def grads_kernel(dec_step, enc_step, depth, block_t, lat_t, err, pgrad, layer_in, enc_out, dec_out, enc_sum, dec_sum, layer_out, dec_buf, enc_buf, sem):
-    layer_out[...] = layer_in[...]
-    jobs = [(0, i) for i in range(dec_out.shape[0] // dec_step)]
-    jobs += [(1, i) for i in range(enc_out.shape[0] // enc_step)]
+def grads_kernel(
+    step, depth, block_t, dec_in, dec_sum_in, pgrad, layer_in, enc_out, dec_out, enc_sum, dec_sum, layer_out, buf, sem, dec_sem,
+):
+    dec_rows = dec_in.shape[0] // 2
+    halves = [
+        pltpu.make_async_copy(
+            dec_in.at[pl.ds(i * dec_rows, dec_rows)], dec_out.at[pl.ds(i * dec_rows, dec_rows)], dec_sem.at[i]
+        )
+        for i in range(2)
+    ]
+    for copy in halves:
+        copy.start()
+    count = enc_out.shape[0] // step
     started = []
-    for k, (kind, i) in enumerate(jobs):
-        x, y, out, buf, step = ((lat_t, err, dec_out, dec_buf, dec_step), (block_t, pgrad, enc_out, enc_buf, enc_step))[kind]
+    for i in range(count):
         slot = i % depth
         if i >= depth:
-            started[k - depth].wait()
+            started[i - depth].wait()
         rows = pl.ds(i * step, step)
-        buf[slot] = jnp.dot(x[rows, :], y[...], preferred_element_type=jnp.float32).astype(jnp.bfloat16)
-        copy = pltpu.make_async_copy(buf.at[slot], out.at[rows], sem.at[kind, slot])
+        buf[slot] = jnp.dot(block_t[rows, :], pgrad[...], preferred_element_type=jnp.float32).astype(jnp.bfloat16)
+        copy = pltpu.make_async_copy(buf.at[slot], enc_out.at[rows], sem.at[slot])
         copy.start()
         started.append(copy)
-    dec_sum[...] = jnp.sum(err[...].astype(jnp.float32), axis=0)
+    layer_out[...] = layer_in[...]
+    dec_sum[...] = dec_sum_in[...]
     enc_sum[...] = jnp.sum(pgrad[...].astype(jnp.float32), axis=0)
-    for k, (kind, i) in enumerate(jobs):
-        count = sum(1 for job in jobs if job[0] == kind)
-        if i >= count - depth:
-            started[k].wait()
-
-
-def grads(block_t, lat_t, err, pgrad, layer_in):
-    width, latents = block_t.shape[0], lat_t.shape[0]
+    for copy in started[max(0, count - depth) :] + halves:
+        copy.wait()
+
+
+def grads(block_t, dec_grad, dec_bias_grad, pgrad, layer_in):
+    width, latents = block_t.shape[0], pgrad.shape[1]
     vmem = pl.BlockSpec(memory_space=pltpu.VMEM)
     hbm = pl.BlockSpec(memory_space=pltpu.HBM)
-    dec_step, enc_step, depth = 1024, 256, 3
+    step, depth = 256, 5
     enc, dec, enc_sum, dec_sum, layer_out = pl.pallas_call(
-        functools.partial(grads_kernel, dec_step, enc_step, depth),
+        functools.partial(grads_kernel, step, depth),
         out_shape=(
             jax.ShapeDtypeStruct((width, latents), jnp.bfloat16),
             jax.ShapeDtypeStruct((latents, width), jnp.bfloat16),
@@ -726,13 +751,13 @@
         in_specs=[vmem] * 5,
         out_specs=(hbm, hbm, vmem, vmem, vmem),
         scratch_shapes=[
-            pltpu.VMEM((depth, dec_step, width), jnp.bfloat16),
-            pltpu.VMEM((depth, enc_step, latents), jnp.bfloat16),
-            pltpu.SemaphoreType.DMA((2, depth)),
+            pltpu.VMEM((depth, step, latents), jnp.bfloat16),
+            pltpu.SemaphoreType.DMA((depth,)),
+            pltpu.SemaphoreType.DMA((2,)),
         ],
-        compiler_params=pltpu.CompilerParams(vmem_limit_bytes=24 * 1024 * 1024),
+        compiler_params=pltpu.CompilerParams(vmem_limit_bytes=16 * 1024 * 1024),
         name="grads",
-    )(block_t, lat_t, err, pgrad, layer_in)
+    )(block_t, dec_grad, dec_bias_grad, pgrad, layer_in)
     return layer_out, enc, enc_sum, dec, dec_sum
 
 
@@ -794,11 +819,11 @@
 ):
     plan = Plan(sizes, query, keys, resid, enc_weight)
     if plan.fits():
-        layer_out, block_t, lat_t, err, pgrad = fused(
+        layer_out, block_t, dec_grad, dec_bias_grad, pgrad = fused(
             plan, query, keys, values, lengths, query_pos, resid, out_weight,
             enc_weight, enc_bias, dec_weight, dec_bias,
         )
-        return grads(block_t, lat_t, err, pgrad, layer_out)
+        return grads(block_t, dec_grad, dec_bias_grad, pgrad, layer_out)
     groups = Groups(sizes)
     row_count = query.shape[0]
     shard_pos = lax.axis_index(("grp", "ctx"))

time: 125 us -> 122 us (0.976)
  Pallas kernels: 121 us -> 118 us
    pallas_call x1, Pallas kernels: 8.06 us -> 6.34 us  [grads(): pl.pallas_call(functools.partial(grads_kernel, step, depth), out_shape=(j...]
where the time goes in v4:
time: 122 us
  Pallas kernels  118 us (97%)
  local copies, waits for them, and re-layouts  1.28 us (1%)
  other arithmetic  1.25 us (1%)
    pallas_call x1, Pallas kernels, fused(): pl.pallas_call(functools.partial(fused_kernel, p), out_shape=(jax.ShapeDt...  112 us
    pallas_call x1, Pallas kernels, grads(): pl.pallas_call(functools.partial(grads_kernel, step, depth), out_shape=(j...  6.34 us

profile of v4, /device:TPU:0, one launch (start us, length us, event | category | flops | bytes accessed | tf_op | source)
XLA Modules:
  0.0 121.8 jit_solution(13000905332451090035)
XLA Ops:
  0.6 0.0 copy-start
  0.7 1.2 copy-done
  1.9 1.2 %maximum_bitcast_fusion = bf16[4,2,64,256]{3,1,2,0:T(2,128)(2,1)S(1)} fusion(bf16[4,64,2,128]{3,2,1,0:T(2,128)(2,1)} %param.13, bf16[4,64,2,128]{3,2,1,0:T(2,128)(2,1)} %param.12), kind=kLoop, calls=%fused_computation | loop fusion | flops 524288 | bytes 524288 | tf_op jit(solution)/shard_map/transpose | solution.py:625
  3.2 112.1 %fused.1 = (bf16[64,640]{1,0:T(8,128)(2,1)S(1)}, bf16[1280,256]{1,0:T(8,128)(2,1)S(1)}, bf16[3072,1280]{1,0:T(8,128)(2,1)S(1)}, f32[1280]{0:T(1024)S(1)}, bf16[256,3072]{1,0:T(8,128)(2,1)S(1)}) custom-call(bf16[2,256,128]{2,1,0:T(8,128)(2,1)S(1)} %bitcast.8, bf16[8,64,256]{2,1,0:T(8,128)(2,1)S(1)} %bitcast.7, s32[4,8]{1,0:T(4,128)} %len_hbm.1, s32[256]{0:T(256)} %pos_hbm.1, ...), custom_call_target="tpu_custom_call" | custom-call | tf_op jit(solution)/shard_map/fused/pallas_call | solution.py:636
  115.3 6.3 %grads.1 = (bf16[1280,3072]{1,0:T(8,128)(2,1)}, bf16[3072,1280]{1,0:T(8,128)(2,1)}, f32[3072]{0:T(1024)}, f32[1280]{0:T(1024)}, bf16[64,640]{1,0:T(8,128)(2,1)}) custom-call(bf16[1280,256]{1,0:T(8,128)(2,1)S(1)} %get-tuple-element.15.block_t, bf16[3072,1280]{1,0:T(8,128)(2,1)S(1)} %get-tuple-element.16.dec_in, f32[1280]{0:T(1024)S(1)} %get-tuple-element.17.dec_sum_in, ...), custom_call_target="tpu_custom_call" | custom-call | tf_op jit(solution)/shard_map/grads/pallas_call | solution.py:742
  (3 shorter events, 0.1 us)
Async XLA Ops:
  0.6 1.2 %copy-start = (bf16[256,16,128]{2,1,0:T(8,128)(2,1)S(1)}, bf16[256,16,128]{2,1,0:T(8,128)(2,1)}, u32[]{:S(2)}) copy-start(bf16[256,16,128]{2,1,0:T(8,128)(2,1)} %param.11) | copy-start | bytes 3145732

commit v5 on v4

--- a/solution.py
+++ b/solution.py
@@ -147,7 +147,7 @@
             and self.cols % 128 == 0
             and self.cols * self.ctx == self.width
             and self.width % (128 * self.cuts) == 0
-            and self.latents % 512 == 0
+            and self.latents % 1024 == 0
             and self.head_dim % 128 == 0
             and self.heads % 2 == 0
         )
@@ -373,70 +373,84 @@
             for j, (lo, hi) in enumerate([(low, high)] + others):
                 arrived(block_at(t, lo, hi, r), blk_cross, (t, i, j, 0))
 
-    def pair_send(k, t):
-        there = part.at[k, rows_at(t * p.rows + (1 - low) * p.half, p.half)]
-        send(there, pair_in.at[k, t], pair_sem, (k, t), partner)
+    lat_half = p.latents // 2
+    spans = [(u, pl.ds(u * lat_half, lat_half)) for u in range(2)]
+
+    def pair_send(k, t, u, cols):
+        there = part.at[k, rows_at(t * p.rows + (1 - low) * p.half, p.half), cols]
+        send(there, pair_in.at[k, t, :, cols], pair_sem, (k, t, u), partner)
 
     def pair_add(k, t):
-        arrived(pair_in.at[k, t], pair_sem, (k, t))
-
-        def body(r):
-            mine = part[k, rows_at(t * p.rows + low * p.half + r, 16)].astype(jnp.float32)
-            pair_sum[k, t, pl.ds(r, 16)] = (mine + pair_in[k, t, pl.ds(r, 16)].astype(jnp.float32)).astype(jnp.bfloat16)
-
-        loop(p.half, body)
+        for u, cols in spans:
+            arrived(pair_in.at[k, t, :, cols], pair_sem, (k, t, u))
+
+            def body(r, cols=cols):
+                mine = part[k, rows_at(t * p.rows + low * p.half + r, 16), cols].astype(jnp.float32)
+                theirs = pair_in[k, t, pl.ds(r, 16), cols].astype(jnp.float32)
+                pair_sum[k, t, pl.ds(r, 16), cols] = (mine + theirs).astype(jnp.bfloat16)
+
+            loop(p.half, body)
+            for s, h in enumerate(highs):
+                send(
+                    pair_sum.at[k, t, rows_at(h * p.quarter, p.quarter), cols], high_in.at[k, t, s, :, cols],
+                    high_sem, (k, t, u, s), to_high(h),
+                )
+
+    def high_sum(k, t, r, cols):
+        total = pair_sum[k, t, rows_at(high * p.quarter + r, 16), cols].astype(jnp.float32)
+        for s in range(len(highs)):
+            total = total + high_in[k, t, s, pl.ds(r, 16), cols].astype(jnp.float32)
+        return total
+
+    def high_wait(k, t, u, cols):
+        for s in range(len(highs)):
+            arrived(high_in.at[k, t, s, :, cols], high_sem, (k, t, u, s))
+
+    def publish(k, t, u, cols, out):
+        mine = out.at[rows_at(quarter_row(t, low, high), p.quarter), cols]
         for s, h in enumerate(highs):
-            send(pair_sum.at[k, t, rows_at(h * p.quarter, p.quarter)], high_in.at[k, t, s], high_sem, (k, t, s), to_high(h))
-
-    def high_sum(k, t, r):
-        total = pair_sum[k, t, rows_at(high * p.quarter + r, 16)].astype(jnp.float32)
-        for s in range(len(highs)):
-            total = total + high_in[k, t, s, pl.ds(r, 16)].astype(jnp.float32)
-        return total
-
-    def publish(k, t, out):
-        mine = out.at[rows_at(quarter_row(t, low, high), p.quarter)]
-        for s, h in enumerate(highs):
-            send(mine, mine, gather_sem, (k, t, s + 1), to_high(h))
-        send(mine, mine, gather_sem, (k, t, 0), partner)
+            send(mine, mine, gather_sem, (k, t, u, s + 1), to_high(h))
+        send(mine, mine, gather_sem, (k, t, u, 0), partner)
 
     def activate(t):
-        for s in range(len(highs)):
-            arrived(high_in.at[0, t, s], high_sem, (0, t, s))
-
-        def body(r):
-            z = 4.0 * (high_sum(0, t, r) + enc_bias[...].reshape(1, -1))
-            e = jnp.exp(-jnp.abs(z))
-            lat[rows_at(quarter_row(t, low, high) + r, 16)] = (
-                (jnp.maximum(z, 0.0) + jnp.log1p(e)) * 0.25
-            ).astype(jnp.bfloat16)
-            factor[t, pl.ds(r, 16)] = jnp.where(z >= 0.0, 1.0, e) / (1.0 + e)
-
-        loop(p.quarter, body)
-        publish(0, t, lat)
+        for u, cols in spans:
+            high_wait(0, t, u, cols)
+
+            def body(r, cols=cols):
+                z = 4.0 * (high_sum(0, t, r, cols) + enc_bias[cols].reshape(1, -1))
+                e = jnp.exp(-jnp.abs(z))
+                lat[rows_at(quarter_row(t, low, high) + r, 16), cols] = (
+                    (jnp.maximum(z, 0.0) + jnp.log1p(e)) * 0.25
+                ).astype(jnp.bfloat16)
+                factor[t, pl.ds(r, 16), cols] = jnp.where(z >= 0.0, 1.0, e) / (1.0 + e)
+
+            loop(p.quarter, body)
+            publish(0, t, u, cols, lat)
 
     def cotangent(t):
-        for s in range(len(highs)):
-            arrived(high_in.at[1, t, s], high_sem, (1, t, s))
-
-        def body(r):
-            pgrad[rows_at(quarter_row(t, low, high) + r, 16)] = (
-                high_sum(1, t, r) * factor[t, pl.ds(r, 16)]
-            ).astype(jnp.bfloat16)
-
-        loop(p.quarter, body)
-        publish(1, t, pgrad)
+        for u, cols in spans:
+            high_wait(1, t, u, cols)
+
+            def body(r, cols=cols):
+                pgrad[rows_at(quarter_row(t, low, high) + r, 16), cols] = (
+                    high_sum(1, t, r, cols) * factor[t, pl.ds(r, 16), cols]
+                ).astype(jnp.bfloat16)
+
+            loop(p.quarter, body)
+            publish(1, t, u, cols, pgrad)
 
     def relay(k, t, out):
-        for s, h in enumerate(highs_from):
-            theirs = out.at[rows_at(quarter_row(t, low, h), p.quarter)]
-            arrived(theirs, gather_sem, (k, t, s + 1))
-            send(theirs, theirs, relay_sem, (k, t, s), partner)
+        for u, cols in spans:
+            for s, h in enumerate(highs_from):
+                theirs = out.at[rows_at(quarter_row(t, low, h), p.quarter), cols]
+                arrived(theirs, gather_sem, (k, t, u, s + 1))
+                send(theirs, theirs, relay_sem, (k, t, u, s), partner)
 
     def collected(k, t, out):
-        arrived(out.at[rows_at(quarter_row(t, 1 - low, high), p.quarter)], gather_sem, (k, t, 0))
-        for s, h in enumerate(highs_from):
-            arrived(out.at[rows_at(quarter_row(t, 1 - low, h), p.quarter)], relay_sem, (k, t, s))
+        for u, cols in spans:
+            arrived(out.at[rows_at(quarter_row(t, 1 - low, high), p.quarter), cols], gather_sem, (k, t, u, 0))
+            for s, h in enumerate(highs_from):
+                arrived(out.at[rows_at(quarter_row(t, 1 - low, h), p.quarter), cols], relay_sem, (k, t, u, s))
 
     def encode(t):
         block_wait(t)
@@ -451,8 +465,9 @@
             ).astype(jnp.bfloat16)
             return carry
 
-        lax.fori_loop(0, enc_steps, step, 0)
-        pair_send(0, t)
+        for u, cols in spans:
+            lax.fori_loop(u * enc_steps // 2, (u + 1) * enc_steps // 2, step, 0)
+            pair_send(0, t, u, cols)
 
     cut = p.width // p.cuts
 
@@ -530,8 +545,9 @@
             ).astype(jnp.bfloat16)
             return carry
 
-        lax.fori_loop(0, enc_steps, step, 0)
-        pair_send(1, t)
+        for u, cols in spans:
+            lax.fori_loop(u * enc_steps // 2, (u + 1) * enc_steps // 2, step, 0)
+            pair_send(1, t, u, cols)
 
     out_step = 512
 
@@ -682,10 +698,10 @@
             dma((2, n, grps)),
             dma((2, n, p.grp)),
             dma((2, n, ctxs, p.wid, p.grp)),
-            dma((2, 2, n)),
-            dma((2, 2, n, highs)),
-            dma((2, 2, n, highs + 1)),
-            dma((2, 2, n, highs)),
+            dma((2, 2, n, 2)),
+            dma((2, 2, n, 2, highs)),
+            dma((2, 2, n, 2, highs + 1)),
+            dma((2, 2, n, 2, highs)),
             dma((2, n, p.cuts, ctxs)),
             dma((2, n, p.cuts, grps)),
             dma((2, n, p.cuts, grps)),

time: 122 us -> 119 us (0.975)
  Pallas kernels: 118 us -> 115 us
    pallas_call x1, Pallas kernels: 112 us -> 109 us  [fused(): pl.pallas_call(functools.partial(fused_kernel, p), out_shape=(jax.ShapeDt...]
where the time goes in v5:
time: 119 us
  Pallas kernels  115 us (97%)
  local copies, waits for them, and re-layouts  1.28 us (1%)
  other arithmetic  1.25 us (1%)
    pallas_call x1, Pallas kernels, fused(): pl.pallas_call(functools.partial(fused_kernel, p), out_shape=(jax.ShapeDt...  109 us
    pallas_call x1, Pallas kernels, grads(): pl.pallas_call(functools.partial(grads_kernel, step, depth), out_shape=(j...  6.34 us

profile of v5, /device:TPU:0, one launch (start us, length us, event | category | flops | bytes accessed | tf_op | source)
XLA Modules:
  0.0 118.7 jit_solution(2921864641312646862)
XLA Ops:
  0.6 0.0 copy-start
  0.7 1.2 %copy-done = bf16[256,16,128]{2,1,0:T(8,128)(2,1)S(1)} copy-done((bf16[256,16,128]{2,1,0:T(8,128)(2,1)S(1)}, bf16[256,16,128]{2,1,0:T(8,128)(2,1)}, u32[]{:S(2)}) %copy-start) | copy-done | bytes 1048600
  1.9 1.2 %maximum_bitcast_fusion = bf16[4,2,64,256]{3,1,2,0:T(2,128)(2,1)S(1)} fusion(bf16[4,64,2,128]{3,2,1,0:T(2,128)(2,1)} %param.13, bf16[4,64,2,128]{3,2,1,0:T(2,128)(2,1)} %param.12), kind=kLoop, calls=%fused_computation | loop fusion | flops 524288 | bytes 524288 | tf_op jit(solution)/shard_map/transpose | solution.py:641
  3.2 109.0 %fused.1 = (bf16[64,640]{1,0:T(8,128)(2,1)S(1)}, bf16[1280,256]{1,0:T(8,128)(2,1)S(1)}, bf16[3072,1280]{1,0:T(8,128)(2,1)S(1)}, f32[1280]{0:T(1024)S(1)}, bf16[256,3072]{1,0:T(8,128)(2,1)S(1)}) custom-call(bf16[2,256,128]{2,1,0:T(8,128)(2,1)S(1)} %bitcast.8, bf16[8,64,256]{2,1,0:T(8,128)(2,1)S(1)} %bitcast.7, s32[4,8]{1,0:T(4,128)} %len_hbm.1, s32[256]{0:T(256)} %pos_hbm.1, ...), custom_call_target="tpu_custom_call" | custom-call | tf_op jit(solution)/shard_map/fused/pallas_call | solution.py:652
  112.2 6.3 %grads.1 = (bf16[1280,3072]{1,0:T(8,128)(2,1)}, bf16[3072,1280]{1,0:T(8,128)(2,1)}, f32[3072]{0:T(1024)}, f32[1280]{0:T(1024)}, bf16[64,640]{1,0:T(8,128)(2,1)}) custom-call(bf16[1280,256]{1,0:T(8,128)(2,1)S(1)} %get-tuple-element.15.block_t, bf16[3072,1280]{1,0:T(8,128)(2,1)S(1)} %get-tuple-element.16.dec_in, f32[1280]{0:T(1024)S(1)} %get-tuple-element.17.dec_sum_in, ...), custom_call_target="tpu_custom_call" | custom-call | tf_op jit(solution)/shard_map/grads/pallas_call | solution.py:758
  (3 shorter events, 0.1 us)
Async XLA Ops:
  0.6 1.2 %copy-start = (bf16[256,16,128]{2,1,0:T(8,128)(2,1)S(1)}, bf16[256,16,128]{2,1,0:T(8,128)(2,1)}, u32[]{:S(2)}) copy-start(bf16[256,16,128]{2,1,0:T(8,128)(2,1)} %param.11) | copy-start | bytes 3145732
